TPU v7x, 256 devices: a whole 4x4x8 slice. The times are simulated.
256 devices in a mesh: gx: 32 (over y, z), gy: 8 (over x, core).
Axes of the slice: x: 4, y: 4, z: 8, core: 2. Of those that a mesh axis runs over, the one named last changes fastest.
Arguments:
- right_side: float32 [64, 128, 4, 3, 128], P('gx', 'gy'), may hold values from -6 to 6
- stencil: float32 [27, 3, 3], replicated, as said below
- class_scale: float32 [8], replicated, may hold values from 0.5 to 4
- material: int32 [64, 128, 128], P('gx', 'gy'), may hold values from 0 to 7
- boundary: int32 [64, 128, 128], P('gx', 'gy'), may hold values 0 or 1
- sign_bits: int32 [64, 128, 3, 128], P('gx', 'gy'), may hold values from 0 to 1
- sample_rows: int32 [32, 8, 128], P('gx', 'gy'), may hold values from 0 to 12287
Outputs:
- solution: float32 [64, 128, 4, 3, 128], P('gx', 'gy')
- residual: float32 [64, 128, 4, 3, 128], P('gx', 'gy')
Inputs may be any that keep to these rules, and one draw needn't show every extreme that they name: In every row of the centre block stencil[13], the diagonal entry exceeds the sum of the magnitudes of all other entries of that row over all 27 blocks.
All inputs are finite; a program needn't handle non-finite values. No bound on the sum of `boundary` on one device may be relied on, other than what follows from the above.
Results may differ from a plain program's by a relative error of at most 0.0028.
Values sent between devices are 32-bit elements; how exact they have to be, the bound alone decides.
A program may use at most 64 MiB of HBM per device.

v0:
```python
import math

import jax
import jax.numpy as jnp
from jax import lax
from jax.sharding import Mesh
from jax.sharding import PartitionSpec as P

STEPS = 8
GX_GY = ("gx_0", "gx_1", "gy_0", "gy_1")
GX = ("gx_0", "gx_1")
GY = ("gy_0", "gy_1")


exact_mode = lax.Precision.HIGHEST


def padded_2(cells, sides, width):
    for axis, dim in sides:
        count = lax.axis_size(axis)
        ends = count - 1
        head = lax.slice_in_dim(cells, 0, width, axis=dim)
        tail = lax.slice_in_dim(cells, cells.shape[dim] - width, cells.shape[dim], axis=dim)
        cells = jnp.concatenate(
            [
                lax.ppermute(tail, axis, [(i, (i + 1) % count) for i in range(ends)]),
                cells,
                lax.ppermute(head, axis, [((i + 1) % count, i) for i in range(ends)]),
            ],
            axis=dim,
        )
    return cells


def one_axis_at_a_time(shard, axes):
    for axis in axes:
        shard = lax.psum(shard, axis)
    return shard


def hadamard_table():
    lanes = jnp.arange(128, dtype=jnp.int32)
    common = lanes[:, None] & lanes[None, :]
    parity = jnp.zeros((128, 128), jnp.int32)
    for bit in range(7):
        parity = parity + (common >> bit & 1)
    return (1 - 2 * (parity % 2)).astype(jnp.float32) / math.sqrt(128.0)


def material_scale(material, class_scale):
    scale_field = jnp.zeros(material.shape, jnp.float32)
    for number in range(class_scale.shape[0]):
        scale_field = scale_field + jnp.where(
            material == number, class_scale[number], jnp.float32(0.0)
        )
    return scale_field


def extend(field):
    return padded_2(field, ((GX, 0), (GY, 1)), 1)


def operate(field, stencil, scale_field, boundary):
    padded = jnp.pad(extend(field), ((0, 0), (0, 0), (0, 0), (0, 0), (1, 1)))
    extent_x, extent_y, extent_z = (field.shape[0], field.shape[1], field.shape[4])
    summed = jnp.zeros(field.shape, jnp.float32)
    for offset_x in range(3):
        for offset_y in range(3):
            for offset_z in range(3):
                shifted = padded[
                    offset_x : offset_x + extent_x,
                    offset_y : offset_y + extent_y,
                    :,
                    :,
                    offset_z : offset_z + extent_z,
                ]
                coupling = stencil[offset_x * 9 + offset_y * 3 + offset_z]
                summed = summed + jnp.sum(
                    coupling[:, :, None] * shifted[:, :, :, None, :, :], axis=4
                )
    return jnp.where(
        boundary[:, :, None, None, :] == 1, field, scale_field[:, :, None, None, :] * summed
    )


def sketch_local(field, sign_field, picks, table):
    pick_x, pick_y, pick_comp, pick_block, pick_lane = picks
    signed = field * sign_field[:, :, None, :, :]
    tiled = signed.reshape(field.shape[:4] + (field.shape[4] // 128, 128))
    chosen = tiled[pick_x, pick_y, :, pick_comp, pick_block]
    return jnp.sum(chosen * table[pick_lane][:, None, :], axis=-1)


def back_substitute(triangle, projected):
    count = triangle.shape[0]

    def one_row(step, unknowns):
        row = count - 1 - step
        line = triangle[row]
        total = jnp.dot(line[None, :], unknowns, precision=exact_mode)[0]
        value = (projected[row] - total) / line[row]
        return unknowns.at[row].set(value)

    return lax.fori_loop(0, count, one_row, jnp.zeros(projected.shape, jnp.float32))


def solve_small(matrix, rhs):
    count = matrix.shape[1]
    columns = matrix.T

    def one_column(column, state_pair):
        orthonormal, triangle = state_pair
        vector = columns[column]
        first_pass = jnp.dot(orthonormal.T, vector, precision=exact_mode)
        vector = vector - jnp.dot(orthonormal, first_pass, precision=exact_mode)
        second_pass = jnp.dot(orthonormal.T, vector, precision=exact_mode)
        vector = vector - jnp.dot(orthonormal, second_pass, precision=exact_mode)
        length = jnp.sqrt(jnp.sum(vector * vector) + 1e-06)
        orthonormal = orthonormal.at[:, column].set(vector / length)
        triangle = triangle.at[:, column].set((first_pass + second_pass).at[column].set(length))
        return (orthonormal, triangle)

    start = (jnp.zeros(matrix.shape, jnp.float32), jnp.zeros((count, count), jnp.float32))
    orthonormal, triangle = lax.fori_loop(0, count, one_column, start)
    projected = jnp.dot(orthonormal.T, rhs, precision=exact_mode)
    return back_substitute(triangle, projected)


def shards(right_side, stencil, class_scale, material, boundary, sign_bits, sample_rows):
    table = hadamard_table()
    scale_field = material_scale(material, class_scale)
    sign_field = (2 * sign_bits - 1).astype(jnp.float32)
    depth = right_side.shape[4]
    plane = right_side.shape[1] * 3 * depth
    sampled = sample_rows[0, 0]
    rest_y = sampled % plane
    rest_c = rest_y % (3 * depth)
    pick_z = rest_c % depth
    picks = (sampled // plane, rest_y // (3 * depth), rest_c // depth, pick_z // 128, pick_z % 128)
    width = right_side.shape[2]
    local_rhs = sketch_local(right_side, sign_field, picks, table)
    sketch_rhs = one_axis_at_a_time(local_rhs, GX_GY)
    lengths = jnp.sqrt(jnp.sum(sketch_rhs * sketch_rhs, axis=0) + 1e-06)
    basis_block = right_side / lengths[None, None, :, None, None]
    sketch_basis = sketch_rhs / lengths
    blocks = []
    sketched_images = []
    for block_step in range(STEPS):
        operated = operate(basis_block, stencil, scale_field, boundary)
        local_image = sketch_local(operated, sign_field, picks, table)
        sketch_image = one_axis_at_a_time(local_image, GX_GY)
        blocks.append(basis_block)
        sketched_images.append(sketch_image)
        if block_step + 1 < STEPS:
            coupling = jnp.dot(sketch_basis.T, sketch_image, precision=exact_mode)
            remainder = operated - jnp.einsum(
                "xyicz,ij->xyjcz", basis_block, coupling, precision=exact_mode
            )
            sketch_remainder = sketch_image - jnp.dot(sketch_basis, coupling, precision=exact_mode)
            norms = jnp.sqrt(jnp.sum(sketch_remainder * sketch_remainder, axis=0) + 1e-06)
            basis_block = remainder / norms[None, None, :, None, None]
            sketch_basis = sketch_remainder / norms
    matrix = jnp.concatenate(sketched_images, axis=1)
    weights = solve_small(matrix, sketch_rhs)
    solution = jnp.zeros(right_side.shape, jnp.float32)
    for block_step in range(STEPS):
        part_weights = weights[block_step * width : (block_step + 1) * width]
        solution = solution + jnp.einsum(
            "xyicz,ij->xyjcz", blocks[block_step], part_weights, precision=exact_mode
        )
    residual = right_side - operate(solution, stencil, scale_field, boundary)
    return (solution, residual)


def solution(mesh):
    split = Mesh(mesh.devices.reshape(4, 8, 4, 2), ("gx_0", "gx_1", "gy_0", "gy_1"))
    return jax.shard_map(
        shards,
        mesh=split,
        in_specs=(
            P(GX, GY, None, None, None),
            P(),
            P(),
            P(GX, GY, None),
            P(GX, GY, None),
            P(GX, GY, None, None),
            P(GX, GY, None),
        ),
        out_specs=(P(GX, GY, None, None, None), P(GX, GY, None, None, None)),
        check_vma=False,
    )
```

profile of v0, /device:TPU:1, one launch (start us, length us, event | category | flops | bytes accessed | tf_op | source)
XLA Modules:
  0.0 820.1 jit_solution(13014205767853807181)
XLA Ops:
  15.6 16.2 %psum.253 = f32[128,4]{0,1:T(4,128)S(1)} all-reduce(f32[128,4]{0,1:T(4,128)S(1)} %psum.252), channel_id=1, replica_groups=mesh['gx_0'=4,'gx_1'=8,'gy_0'=4,'gy_1'=2] {'gx_1'}, use_global_device_ids=true, to_apply=%region_2.3 | all-reduce | flops 512 | bytes 4096 | tf_op jit(solution)/shard_map/psum | solution.py:37
  81.0 12.5 %psum.257 = f32[128,4]{0,1:T(4,128)S(1)} all-reduce(f32[128,4]{0,1:T(4,128)S(1)} %psum.256), channel_id=1, replica_groups=mesh['gx_0'=4,'gx_1'=8,'gy_0'=4,'gy_1'=2] {'gx_1'}, use_global_device_ids=true, to_apply=%region_35.36 | all-reduce | flops 512 | bytes 4096 | tf_op jit(solution)/shard_map/psum | solution.py:37
  99.5 11.7 %psum.259 = f32[128,4]{0,1:T(4,128)S(1)} all-reduce(f32[128,4]{0,1:T(4,128)S(1)} %psum.258), channel_id=1, replica_groups=mesh['gx_0'=4,'gx_1'=8,'gy_0'=4,'gy_1'=2] {'gy_1'}, use_global_device_ids=true, to_apply=%region_37.38 | all-reduce | flops 512 | bytes 4096 | tf_op jit(solution)/shard_map/psum | solution.py:37
  132.0 10.7 %psum.260 = f32[128,4]{0,1:T(4,128)S(1)} all-reduce(f32[128,4]{0,1:T(4,128)S(1)} %copy.1905), channel_id=1, replica_groups=mesh['gx_0'=4,'gx_1'=8,'gy_0'=4,'gy_1'=2] {'gx_0'}, use_global_device_ids=true, to_apply=%region_67.68 | all-reduce | flops 512 | bytes 4096 | tf_op jit(solution)/shard_map/psum | solution.py:37
  142.7 10.7 %psum.261 = f32[128,4]{0,1:T(4,128)S(1)} all-reduce(f32[128,4]{0,1:T(4,128)S(1)} %psum.260), channel_id=1, replica_groups=mesh['gx_0'=4,'gx_1'=8,'gy_0'=4,'gy_1'=2] {'gx_1'}, use_global_device_ids=true, to_apply=%region_68.69 | all-reduce | flops 512 | bytes 4096 | tf_op jit(solution)/shard_map/psum | solution.py:37
  159.7 11.7 %psum.263 = f32[128,4]{0,1:T(4,128)S(1)} all-reduce(f32[128,4]{0,1:T(4,128)S(1)} %psum.262), channel_id=1, replica_groups=mesh['gx_0'=4,'gx_1'=8,'gy_0'=4,'gy_1'=2] {'gy_1'}, use_global_device_ids=true, to_apply=%region_70.71 | all-reduce | flops 512 | bytes 4096 | tf_op jit(solution)/shard_map/psum | solution.py:37
  192.6 11.2 %psum.264 = f32[128,4]{0,1:T(4,128)S(1)} all-reduce(f32[128,4]{0,1:T(4,128)S(1)} %copy.1910), channel_id=1, replica_groups=mesh['gx_0'=4,'gx_1'=8,'gy_0'=4,'gy_1'=2] {'gx_0'}, use_global_device_ids=true, to_apply=%region_100.101 | all-reduce | flops 512 | bytes 4096 | tf_op jit(solution)/shard_map/psum | solution.py:37
  203.8 10.7 %psum.265 = f32[128,4]{0,1:T(4,128)S(1)} all-reduce(f32[128,4]{0,1:T(4,128)S(1)} %psum.264), channel_id=1, replica_groups=mesh['gx_0'=4,'gx_1'=8,'gy_0'=4,'gy_1'=2] {'gx_1'}, use_global_device_ids=true, to_apply=%region_101.102 | all-reduce | flops 512 | bytes 4096 | tf_op jit(solution)/shard_map/psum | solution.py:37
  220.5 11.7 %psum.267 = f32[128,4]{0,1:T(4,128)S(1)} all-reduce(f32[128,4]{0,1:T(4,128)S(1)} %psum.266), channel_id=1, replica_groups=mesh['gx_0'=4,'gx_1'=8,'gy_0'=4,'gy_1'=2] {'gy_1'}, use_global_device_ids=true, to_apply=%region_103.104 | all-reduce | flops 512 | bytes 4096 | tf_op jit(solution)/shard_map/psum | solution.py:37
  253.4 11.2 %psum.268 = f32[128,4]{0,1:T(4,128)S(1)} all-reduce(f32[128,4]{0,1:T(4,128)S(1)} %copy.1915), channel_id=1, replica_groups=mesh['gx_0'=4,'gx_1'=8,'gy_0'=4,'gy_1'=2] {'gx_0'}, use_global_device_ids=true, to_apply=%region_133.134 | all-reduce | flops 512 | bytes 4096 | tf_op jit(solution)/shard_map/psum | solution.py:37
  264.6 10.7 %psum.269 = f32[128,4]{0,1:T(4,128)S(1)} all-reduce(f32[128,4]{0,1:T(4,128)S(1)} %psum.268), channel_id=1, replica_groups=mesh['gx_0'=4,'gx_1'=8,'gy_0'=4,'gy_1'=2] {'gx_1'}, use_global_device_ids=true, to_apply=%region_134.135 | all-reduce | flops 512 | bytes 4096 | tf_op jit(solution)/shard_map/psum | solution.py:37
  281.4 11.7 %psum.271 = f32[128,4]{0,1:T(4,128)S(1)} all-reduce(f32[128,4]{0,1:T(4,128)S(1)} %psum.270), channel_id=1, replica_groups=mesh['gx_0'=4,'gx_1'=8,'gy_0'=4,'gy_1'=2] {'gy_1'}, use_global_device_ids=true, to_apply=%region_136.137 | all-reduce | flops 512 | bytes 4096 | tf_op jit(solution)/shard_map/psum | solution.py:37
  314.2 11.2 %psum.272 = f32[128,4]{0,1:T(4,128)S(1)} all-reduce(f32[128,4]{0,1:T(4,128)S(1)} %copy.1920), channel_id=1, replica_groups=mesh['gx_0'=4,'gx_1'=8,'gy_0'=4,'gy_1'=2] {'gx_0'}, use_global_device_ids=true, to_apply=%region_166.167 | all-reduce | flops 512 | bytes 4096 | tf_op jit(solution)/shard_map/psum | solution.py:37
  325.4 10.7 %psum.273 = f32[128,4]{0,1:T(4,128)S(1)} all-reduce(f32[128,4]{0,1:T(4,128)S(1)} %psum.272), channel_id=1, replica_groups=mesh['gx_0'=4,'gx_1'=8,'gy_0'=4,'gy_1'=2] {'gx_1'}, use_global_device_ids=true, to_apply=%region_167.168 | all-reduce | flops 512 | bytes 4096 | tf_op jit(solution)/shard_map/psum | solution.py:37
  342.2 11.7 %psum.275 = f32[128,4]{0,1:T(4,128)S(1)} all-reduce(f32[128,4]{0,1:T(4,128)S(1)} %psum.274), channel_id=1, replica_groups=mesh['gx_0'=4,'gx_1'=8,'gy_0'=4,'gy_1'=2] {'gy_1'}, use_global_device_ids=true, to_apply=%region_169.170 | all-reduce | flops 512 | bytes 4096 | tf_op jit(solution)/shard_map/psum | solution.py:37
  375.0 11.2 %psum.276 = f32[128,4]{0,1:T(4,128)S(1)} all-reduce(f32[128,4]{0,1:T(4,128)S(1)} %copy.1925), channel_id=1, replica_groups=mesh['gx_0'=4,'gx_1'=8,'gy_0'=4,'gy_1'=2] {'gx_0'}, use_global_device_ids=true, to_apply=%region_199.200 | all-reduce | flops 512 | bytes 4096 | tf_op jit(solution)/shard_map/psum | solution.py:37
  386.2 10.7 %psum.277 = f32[128,4]{0,1:T(4,128)S(1)} all-reduce(f32[128,4]{0,1:T(4,128)S(1)} %psum.276), channel_id=1, replica_groups=mesh['gx_0'=4,'gx_1'=8,'gy_0'=4,'gy_1'=2] {'gx_1'}, use_global_device_ids=true, to_apply=%region_200.201 | all-reduce | flops 512 | bytes 4096 | tf_op jit(solution)/shard_map/psum | solution.py:37
  402.9 11.7 %psum.279 = f32[128,4]{0,1:T(4,128)S(1)} all-reduce(f32[128,4]{0,1:T(4,128)S(1)} %psum.278), channel_id=1, replica_groups=mesh['gx_0'=4,'gx_1'=8,'gy_0'=4,'gy_1'=2] {'gy_1'}, use_global_device_ids=true, to_apply=%region_202.203 | all-reduce | flops 512 | bytes 4096 | tf_op jit(solution)/shard_map/psum | solution.py:37
  435.8 11.2 %psum.280 = f32[128,4]{0,1:T(4,128)S(1)} all-reduce(f32[128,4]{0,1:T(4,128)S(1)} %copy.1930), channel_id=1, replica_groups=mesh['gx_0'=4,'gx_1'=8,'gy_0'=4,'gy_1'=2] {'gx_0'}, use_global_device_ids=true, to_apply=%region_232.233 | all-reduce | flops 512 | bytes 4096 | tf_op jit(solution)/shard_map/psum | solution.py:37
  463.7 11.7 %psum.283 = f32[128,4]{0,1:T(4,128)S(1)} all-reduce(f32[128,4]{0,1:T(4,128)S(1)} %psum.282), channel_id=1, replica_groups=mesh['gx_0'=4,'gx_1'=8,'gy_0'=4,'gy_1'=2] {'gy_1'}, use_global_device_ids=true, to_apply=%region_235.236 | all-reduce | flops 512 | bytes 4096 | tf_op jit(solution)/shard_map/psum | solution.py:37
  496.6 11.2 %psum.284 = f32[128,4]{0,1:T(4,128)S(1)} all-reduce(f32[128,4]{0,1:T(4,128)S(1)} %copy.1935), channel_id=1, replica_groups=mesh['gx_0'=4,'gx_1'=8,'gy_0'=4,'gy_1'=2] {'gx_0'}, use_global_device_ids=true, to_apply=%region_265.266 | all-reduce | flops 512 | bytes 4096 | tf_op jit(solution)/shard_map/psum | solution.py:37
  524.5 11.7 %psum.287 = f32[128,4]{0,1:T(4,128)S(1)} all-reduce(f32[128,4]{0,1:T(4,128)S(1)} %psum.286), channel_id=1, replica_groups=mesh['gx_0'=4,'gx_1'=8,'gy_0'=4,'gy_1'=2] {'gy_1'}, use_global_device_ids=true, to_apply=%region_268.269 | all-reduce | flops 512 | bytes 4096 | tf_op jit(solution)/shard_map/psum | solution.py:37
  536.3 173.4 %while.35 = (s32[]{:T(128)}, f32[128,32]{0,1:T(8,128)S(1)}, f32[32,32]{0,1:T(8,128)S(1)}, f32[32,128]{1,0:T(8,128)S(1)}, s32[]{:T(128)}, /*index=5*/s32[1]{0:T(128)}, f32[]{:T(128)}, s32[]{:T(128)}, s32[1]{0:T(128)}) while((s32[]{:T(128)}, f32[128,32]{0,1:T(8,128)S(1)}, f32[32,32]{0,1:T(8,128)S(1)}, f32[32,128]{1,0:T(8,128)S(1)}, ...), condition=%wide.region_272.273_spmd, body=%wide.region_269.272_spmd.sunk | while | flops 197457 | bytes 72798 | solution.py:124
  709.9 85.4 %while.36 = (s32[]{:T(128)}, f32[32,4]{1,0:T(8,128)S(1)}, f32[32,4]{1,0:T(8,128)S(1)}, f32[32,32]{1,0:T(8,128)S(1)}, s32[]{:T(128)}, /*index=5*/s32[2]{0:T(128)S(1)}, s32[1]{0:T(128)}, s32[]{:T(128)}, s32[]{:T(128)}, s32[]{:T(128)}) while((s32[]{:T(128)}, f32[32,4]{1,0:T(8,128)S(1)}, f32[32,4]{1,0:T(8,128)S(1)}, ...), condition=%wide.region_275.276_spmd, body=%wide.region_273.275_spmd.sunk | while | flops 1564 | bytes 20220 | solution.py:104
  (993 shorter events, 518.2 us)
Async XLA Ops:
  51.1 11.7 %collective-permute-start.1 = (f32[1,16,4,3,128]{4,1,3,2,0:T(8,128)S(1)}, f32[1,16,4,3,128]{4,1,3,2,0:T(8,128)S(1)}, u32[]{:S(2)}, u32[]{:S(2)}) collective-permute-start(f32[1,16,4,3,128]{4,1,3,2,0:T(8,128)S(1)} %get-tuple-element.683), channel_id=1, source_target_pairs={{8,0},{16,8},{24,16},{32,24},{40,32},{48,40},{56,48},{64,56},{72,6... | collective-permute-start | bytes 294920 | tf_op jit(solution)/shard_map/ppermute | solution.py:28
  52.4 10.4 %collective-permute-start = (f32[1,16,4,3,128]{4,1,3,2,0:T(8,128)S(1)}, f32[1,16,4,3,128]{4,1,3,2,0:T(8,128)S(1)}, u32[]{:S(2)}, u32[]{:S(2)}) collective-permute-start(f32[1,16,4,3,128]{4,1,3,2,0:T(8,128)S(1)} %get-tuple-element.682), channel_id=1, source_target_pairs={{0,8},{8,16},{16,24},{24,32},{32,40},{40,48},{48,56},{56,64},{64,7... | collective-permute-start | bytes 294920 | tf_op jit(solution)/shard_map/ppermute | solution.py:26
  112.5 5.9 collective-permute-start.5
  119.4 6.4 collective-permute-start.7
  172.7 6.5 collective-permute-start.9
  174.0 6.1 collective-permute-start.8
  180.1 5.8 collective-permute-start.11
  233.5 6.5 collective-permute-start.13
  234.8 6.1 collective-permute-start.12
  240.9 6.0 collective-permute-start.15
  294.3 6.5 collective-permute-start.17
  295.6 6.1 collective-permute-start.16
  301.7 5.8 collective-permute-start.19
  355.1 6.5 collective-permute-start.21
  356.4 6.1 collective-permute-start.20
  362.5 6.1 collective-permute-start.23
  415.9 6.5 collective-permute-start.25
  417.2 6.1 collective-permute-start.24
  476.7 6.5 collective-permute-start.29
  478.0 6.1 collective-permute-start.28
  484.1 6.1 collective-permute-start.31
  800.4 6.4 collective-permute-start.33
  801.7 6.0 collective-permute-start.32
  807.8 6.1 collective-permute-start.35
  (18 other events, 520.6 us)
where the time goes:
time: 833 us; the launch traced here: 820 us
  blocking collectives  358 us (43%)
  other arithmetic  135 us (16%)
  starting transfers between devices  101 us (12%)
  matrix products  92.9 us (11%)
  local copies, waits for them, and re-layouts  67.1 us (8%)
  loops' own time  44.2 us (5%)
  waiting for transfers between devices  17.9 us (2%)
    psum x36, blocking collectives, one_axis_at_a_time(): shard = lax.psum(shard, axis)  358 us
    another operation x128, other arithmetic  87.4 us
    ppermute x18, starting transfers between devices, padded_2(): lax.ppermute(tail, axis, [(i, (i + 1) % count) for i in range(ends)])  61.4 us
    another operation x1, loops' own time, solve_small(): orthonormal, triangle = lax.fori_loop(0, count, one_column, start)  43.5 us
    dot_general x32, matrix products, one_row(): total = jnp.dot(line[None, :], unknowns, precision=exact_mode)[0]  42.8 us
    ppermute x18, starting transfers between devices, padded_2(): lax.ppermute(head, axis, [((i + 1) % count, i) for i in range(ends)])  39.6 us
    dot_general x32, matrix products, one_column(): vector = vector - jnp.dot(orthonormal, second_pass, precision=exact_mode)  25.2 us
    reduce_sum x230, other arithmetic, operate(): jnp.sum(coupling[:, :, None] * shifted[:, :, :, None, :, :], axis=4)  25 us
  transfers between devices with their start and end apart: 36, of which 25 were waited for; matrix products, arithmetic and copies ran while one was open for 1% of the time, Pallas kernels for 0%

commit v1 on v0

v1 whole, which is shorter than its diff:
```python
import numpy as np
import jax
import jax.numpy as jnp
from jax import lax
from jax.experimental import pallas as pl
from jax.experimental.pallas import tpu as pltpu
from jax.sharding import PartitionSpec as P

STEPS = 8
NV = STEPS + 1
BW = 4
NROW = NV * BW
HIGH = lax.Precision.HIGHEST
MESH = pl.DeviceIdType.MESH

ROW0 = 8


def phase_tables():
    points = [
        (x * np.pi / 3, y * np.pi / 2, z * np.pi / 4)
        for x in range(4)
        for y in range(4)
        for z in range(8)
    ]
    offsets = [(o // 9 - 1, (o // 3) % 3 - 1, o % 3 - 1) for o in range(27)]
    phase = np.zeros((32, 128))
    phase[:27] = np.array(offsets) @ np.array(points).T
    keep = (np.arange(32) < 27)[:, None]
    return (np.cos(phase) * keep).astype(np.float32), (np.sin(phase) * keep).astype(np.float32)


def neighbours(n_gx, n_gy):
    gx, gy = lax.axis_index("gx"), lax.axis_index("gy")
    out = []
    for dx in (-1, 0, 1):
        for dy in (-1, 0, 1):
            if dx == 0 and dy == 0:
                continue
            ok = jnp.bool_(True)
            if dx < 0:
                ok = jnp.logical_and(ok, gx > 0)
            if dx > 0:
                ok = jnp.logical_and(ok, gx < n_gx - 1)
            if dy < 0:
                ok = jnp.logical_and(ok, gy > 0)
            if dy > 0:
                ok = jnp.logical_and(ok, gy < n_gy - 1)
            out.append((dx, dy, ok, {"gx": gx + dx, "gy": gy + dy}))
    return out


def spectrum(cos_ref, sin_ref, coef_ref, scale_ref):
    contract = (((0,), (0,)), ((), ()))
    coef = coef_ref[...]
    re = lax.dot_general(coef, cos_ref[...], contract, precision=HIGH, preferred_element_type=jnp.float32)
    im = lax.dot_general(coef, sin_ref[...], contract, precision=HIGH, preferred_element_type=jnp.float32)

    def row(t, i, j):
        return t[3 * i + j : 3 * i + j + 1]

    low, high = None, None
    for i in range(3):
        off = jnp.zeros((1, 128), jnp.float32)
        for j in range(3):
            if j != i:
                a = 0.5 * (row(re, i, j) + row(re, j, i))
                b = 0.5 * (row(im, i, j) - row(im, j, i))
                off = off + jnp.sqrt(a * a + b * b)
        lo, hi = row(re, i, i) - off, row(re, i, i) + off
        low = lo if low is None else jnp.minimum(low, lo)
        high = hi if high is None else jnp.maximum(high, hi)
    low = jnp.min(low, axis=1, keepdims=True)
    high = jnp.max(high, axis=1, keepdims=True)
    scales = scale_ref[0:1, :]
    smin = jnp.min(scales, axis=1, keepdims=True)
    smax = jnp.max(scales, axis=1, keepdims=True)
    low = jnp.minimum(jnp.minimum(low * smin, low * smax), 1.0)
    high = jnp.maximum(high * smax, 1.0)
    span = high - low
    low, high = low + 0.04 * span, high - 0.2 * span
    centre = 0.5 * (low + high)
    half = jnp.maximum(0.5 * (high - low), 1e-3 * high)
    return centre, half


def basis_kernel(
    n_gx, n_gy,
    stencil_ref, rhs_ref, factor_ref, signs_ref, sample_ref, cos_ref, sin_ref, coef_ref, scale_ref,
    basis_ref, sketch_ref, shape_ref,
    v, alpha, beta, mask, signed, send_sem, recv_sem, out_sem,
):
    around = neighbours(n_gx, n_gy)
    barrier = pltpu.get_barrier_semaphore()
    count = jnp.int32(0)
    for dx, dy, ok, device in around:
        count = count + jnp.where(ok, 1, 0)

        @pl.when(ok)
        def _():
            pl.semaphore_signal(barrier, inc=1, device_id=device, device_id_type=MESH)

    gx, gy = lax.axis_index("gx"), lax.axis_index("gy")

    v[0, :, :, 1:3, ROW0 : ROW0 + 16, :] = rhs_ref[...]

    def clear(k, carry):
        @pl.when(gx == 0)
        def _():
            v[k, :, :, 0] = jnp.zeros((BW, 3, 32, 128), jnp.float32)

        @pl.when(gx == n_gx - 1)
        def _():
            v[k, :, :, 3] = jnp.zeros((BW, 3, 32, 128), jnp.float32)

        @pl.when(gy == 0)
        def _():
            v[k, :, :, :, ROW0 - 1 : ROW0, :] = jnp.zeros((BW, 3, 4, 1, 128), jnp.float32)

        @pl.when(gy == n_gy - 1)
        def _():
            v[k, :, :, :, ROW0 + 16 : ROW0 + 17, :] = jnp.zeros((BW, 3, 4, 1, 128), jnp.float32)

        return carry

    lax.fori_loop(0, STEPS, clear, 0)
    pl.semaphore_wait(barrier, count)

    def halo(k, part, n):
        dx, dy, ok, device = around[n]
        xs = {-1: (1, 1, 3), 0: (1, 2, 1), 1: (2, 1, 0)}[dx]
        ys = {-1: (ROW0, 1, ROW0 + 16), 0: (ROW0, 16, ROW0), 1: (ROW0 + 15, 1, ROW0 - 1)}[dy]
        cols = pl.ds(2 * part, 2)
        return pltpu.make_async_remote_copy(
            src_ref=v.at[k, cols, :, pl.ds(xs[0], xs[1]), pl.ds(ys[0], ys[1]), :],
            dst_ref=v.at[k, cols, :, pl.ds(xs[2], xs[1]), pl.ds(ys[2], ys[1]), :],
            send_sem=send_sem.at[k, part, n],
            recv_sem=recv_sem.at[k, part, n],
            device_id=device,
            device_id_type=MESH,
        )

    def start(k, part):
        for n in range(8):
            @pl.when(around[n][2])
            def _():
                halo(k, part, n).start()

    def opposite(n):
        return 7 - n

    def arrive(k, part):
        for n in range(8):
            @pl.when(around[n][2])
            def _():
                halo(k, part, opposite(n)).wait_recv()

    def sent(k, part):
        for n in range(8):
            @pl.when(around[n][2])
            def _():
                halo(k, part, n).wait_send()

    start(0, 0)
    start(0, 1)

    centre, half = spectrum(cos_ref, sin_ref, coef_ref, scale_ref)
    inverse = 1.0 / half
    shape_ref[0:1, :] = jnp.broadcast_to(centre * inverse, (1, 128))
    shape_ref[1:2, :] = jnp.broadcast_to(inverse, (1, 128))
    shape_ref[2:8, :] = jnp.zeros((6, 128), jnp.float32)
    factor = factor_ref[...]
    inv3 = inverse.reshape(1, 1, 1)
    cen3 = centre.reshape(1, 1, 1)
    alpha[...] = factor * (2.0 * inv3)
    beta[...] = jnp.where(factor == 0.0, 2.0 * (1.0 - cen3), -2.0 * cen3) * inv3

    sample = sample_ref[...]
    piece = sample >> 7
    lane = sample & 127
    px = jnp.where(piece >= 48, 1, 0)
    rest = piece - 48 * px
    py = (rest * 171) >> 9
    pc = rest - 3 * py
    mine = pc * 32 + px * 16 + py
    pieces = lax.broadcasted_iota(jnp.int32, (96, 128), 0)
    chosen = jnp.where(pieces == mine, 1.0, 0.0)
    mask[...] = chosen
    common = lax.broadcasted_iota(jnp.int32, (128, 128), 0) & lane
    common = common ^ (common >> 4)
    common = common ^ (common >> 2)
    common = common ^ (common >> 1)
    hadamard = (1 - 2 * (common & 1)).astype(jnp.float32)
    signs = (2 * signs_ref[...] - 1).astype(jnp.float32).reshape(96, 128)
    picked = lax.dot_general(
        signs, chosen, (((0,), (0,)), ((), ())), precision=HIGH, preferred_element_type=jnp.float32
    )
    signed[...] = hadamard * picked

    def sketch(k):
        rows = []
        for b in range(BW):
            block = v[k, b, :, 1:3, ROW0 : ROW0 + 16, :].reshape(96, 128)
            spread = jnp.dot(block, signed[...], precision=HIGH, preferred_element_type=jnp.float32)
            rows.append(jnp.sum(spread * mask[...], axis=0, keepdims=True))
        rows = jnp.concatenate(rows, axis=0) * np.float32(1.0 / np.sqrt(128.0))
        sketch_ref[k] = rows

    def keep(k):
        return pltpu.make_async_copy(
            v.at[k, :, :, pl.ds(1, 2), pl.ds(ROW0, 16), :], basis_ref.at[k], out_sem.at[k]
        )

    keep(0).start()
    sketch(0)

    z_lane = lax.broadcasted_iota(jnp.int32, (1, 1, 1, 128), 3)
    not_last = z_lane < 127
    not_first = z_lane > 0

    def step(k, carry):
        first = k == 0
        own = jnp.where(first, jnp.float32(0.5), jnp.float32(1.0))
        old = jnp.where(first, jnp.float32(0.0), jnp.float32(1.0))
        before = jnp.maximum(k - 1, 0)
        for part in range(2):
            arrive(k, part)
            cols = pl.ds(2 * part, 2)
            total = [None, None, None]
            for dz in (-1, 1, 0):
                acc = list(total) if dz == 0 else [None, None, None]
                for dx in (-1, 0, 1):
                    for dy in (-1, 0, 1):
                        offset = 9 * (dx + 1) + 3 * (dy + 1) + (dz + 1)
                        for j in range(3):
                            field = v[k, cols, j, pl.ds(1 + dx, 2), pl.ds(ROW0 + dy, 16), :]
                            for i in range(3):
                                term = stencil_ref[offset * 9 + 3 * i + j] * field
                                acc[i] = term if acc[i] is None else acc[i] + term
                for i in range(3):
                    if dz == -1:
                        moved = jnp.where(not_first, pltpu.roll(acc[i], 1, 3), 0.0)
                        total[i] = moved
                    elif dz == 1:
                        moved = jnp.where(not_last, pltpu.roll(acc[i], 127, 3), 0.0)
                        total[i] = total[i] + moved
                    else:
                        total[i] = acc[i]
            for i in range(3):
                mid = v[k, cols, i, 1:3, ROW0 : ROW0 + 16, :]
                last = v[before, cols, i, 1:3, ROW0 : ROW0 + 16, :]
                value = own * (alpha[...] * total[i] + beta[...] * mid) - old * last
                v[k + 1, cols, i, 1:3, ROW0 : ROW0 + 16, :] = value

            @pl.when(k + 1 < STEPS)
            def _():
                start(k + 1, part)

        keep(k + 1).start()
        sketch(k + 1)
        for part in range(2):
            sent(k, part)
        return carry

    lax.fori_loop(0, STEPS, step, 0)

    def finish(k, carry):
        keep(k).wait()
        return carry

    lax.fori_loop(0, NV, finish, 0)


def solve_kernel(table_ref, shape_ref, basis_ref, solution_ref, residual_ref, rows, weights, sem):
    table = table_ref[...]
    ratio = shape_ref[0:1, 0:1]
    inverse = shape_ref[1:2, :]

    def block(k):
        return table[BW * k : BW * (k + 1)]

    images = [ratio * block(0) + block(1)]
    for k in range(1, STEPS):
        images.append(ratio * block(k) + 0.5 * (block(k + 1) + block(k - 1)))
    q = jnp.concatenate(images + [block(0)], axis=0)
    r = lax.broadcasted_iota(jnp.int32, (NROW, 128), 0)
    l = lax.broadcasted_iota(jnp.int32, (NROW, 128), 1)
    low = r < BW
    last = r >= BW * STEPS
    one, none = jnp.float32(1.0), jnp.float32(0.0)
    e = jnp.where(l == r, ratio, none)
    e = e + jnp.where(l == r + BW, jnp.where(low, one, 0.5), none)
    e = e + jnp.where(jnp.logical_and(l == r - BW, jnp.logical_not(low)), 0.5, none)
    e = e + jnp.where(l == r + 64, one, none)
    e = jnp.where(last, jnp.where(l == r - BW * STEPS, one, none), e)
    size = jnp.sum(q * q, axis=1, keepdims=True)
    unit = jnp.where(last[:, 0:1], one, lax.rsqrt(size + 1e-30))
    q = q * unit
    e = e * unit
    row = r[:, 0:1]
    weight = []
    for j in range(BW * STEPS):
        pivot = q[j : j + 1]
        dots = jnp.sum(q * pivot, axis=1, keepdims=True)
        scale = 1.0 / (dots[j : j + 1] + 1e-10)
        weight.append(scale)
        part = jnp.where(row > j, dots * scale, none)
        q = q - part * pivot
        e = e - part * e[j : j + 1]
    weight = jnp.concatenate(weight, axis=0)
    qs = q[: BW * STEPS]
    es = e[: BW * STEPS] * weight
    last_rows = e[BW * STEPS :]
    for _ in range(2):
        left = jnp.dot(last_rows[:, :NROW], table, precision=HIGH, preferred_element_type=jnp.float32)
        along = lax.dot_general(
            left, qs, (((1,), (1,)), ((), ())), precision=HIGH, preferred_element_type=jnp.float32
        )
        last_rows = last_rows - jnp.dot(along, es, precision=HIGH, preferred_element_type=jnp.float32)
    rows[0:BW] = last_rows
    rows[BW : 2 * BW] = -inverse * last_rows
    copy = pltpu.make_async_copy(rows, weights, sem)
    copy.start()
    copy.wait()
    for x in range(2):
        for b in range(BW):
            sol = jnp.zeros((3, 16, 128), jnp.float32)
            res = jnp.zeros((3, 16, 128), jnp.float32)
            for k in range(NV):
                for a in range(BW):
                    field = basis_ref[k, a, :, x]
                    res = res + weights[b, BW * k + a] * field
                    if k < STEPS:
                        sol = sol + weights[BW + b, 64 + BW * k + a] * field
            solution_ref[b, :, x] = sol
            residual_ref[b, :, x] = res


def solution(mesh):
    n_gx, n_gy = mesh.shape["gx"], mesh.shape["gy"]
    cosine, sine = phase_tables()

    def shards(right_side, stencil, class_scale, material, boundary, sign_bits, sample_rows):
        rhs = jnp.transpose(right_side, (2, 3, 0, 1, 4))
        signs = jnp.transpose(sign_bits, (2, 0, 1, 3))
        field = jnp.zeros(material.shape, jnp.float32)
        for number in range(class_scale.shape[0]):
            field = jnp.where(material == number, class_scale[number], field)
        factor = jnp.where(boundary == 1, jnp.float32(0.0), field)
        coef = jnp.pad(stencil.reshape(27, 9), ((0, 5), (0, 7)))
        scales = jnp.broadcast_to(jnp.tile(class_scale, 16)[None, :], (8, 128))
        vmem = pl.BlockSpec(memory_space=pltpu.VMEM)
        smem = pl.BlockSpec(memory_space=pltpu.SMEM)
        basis, sketch, shape = pl.pallas_call(
            lambda *refs: basis_kernel(n_gx, n_gy, *refs),
            out_shape=(
                jax.ShapeDtypeStruct((NV, BW, 3, 2, 16, 128), jnp.float32),
                jax.ShapeDtypeStruct((NV, BW, 128), jnp.float32),
                jax.ShapeDtypeStruct((8, 128), jnp.float32),
            ),
            in_specs=[smem] + [vmem] * 8,
            out_specs=(pl.BlockSpec(memory_space=pl.ANY), vmem, vmem),
            scratch_shapes=[
                pltpu.VMEM((NV, BW, 3, 4, 32, 128), jnp.float32),
                pltpu.VMEM((2, 16, 128), jnp.float32),
                pltpu.VMEM((2, 16, 128), jnp.float32),
                pltpu.VMEM((96, 128), jnp.float32),
                pltpu.VMEM((128, 128), jnp.float32),
                pltpu.SemaphoreType.DMA((STEPS, 2, 8)),
                pltpu.SemaphoreType.DMA((STEPS, 2, 8)),
                pltpu.SemaphoreType.DMA((NV,)),
            ],
            compiler_params=pltpu.CompilerParams(collective_id=0, has_side_effects=True),
            name="basis",
        )(stencil.reshape(-1), rhs, factor, signs, sample_rows.reshape(1, 128), cosine, sine, coef, scales)
        table = lax.psum(sketch.reshape(NROW, 128), ("gx", "gy"))
        out = jax.ShapeDtypeStruct((BW, 3, 2, 16, 128), jnp.float32)
        answer, residual = pl.pallas_call(
            solve_kernel,
            out_shape=(out, out),
            in_specs=[vmem] * 3,
            out_specs=(vmem, vmem),
            scratch_shapes=[
                pltpu.VMEM((8, 128), jnp.float32),
                pltpu.SMEM((8, 128), jnp.float32),
                pltpu.SemaphoreType.DMA,
            ],
            name="solve",
        )(table, shape, basis)
        back = lambda t: jnp.transpose(t, (2, 3, 0, 1, 4))
        return back(answer), back(residual)

    return jax.shard_map(
        shards,
        mesh=mesh,
        in_specs=(
            P("gx", "gy", None, None, None),
            P(),
            P(),
            P("gx", "gy", None),
            P("gx", "gy", None),
            P("gx", "gy", None, None),
            P("gx", "gy", None),
        ),
        out_specs=(P("gx", "gy", None, None, None), P("gx", "gy", None, None, None)),
        check_vma=False,
    )
```

time: 833 us -> 159 us (0.19); the launches traced: 820 us -> 159 us
  blocking collectives: 358 us -> 82 us
  other arithmetic: 135 us -> 6.24 us
  starting transfers between devices: 101 us -> 0 us
  matrix products: 92.9 us -> 0 us
  Pallas kernels: 0 us -> 56.8 us
  local copies, waits for them, and re-layouts: 67.1 us -> 13.2 us
  loops' own time: 44.2 us -> 0 us
  waiting for transfers between devices: 17.9 us -> 0 us
    psum x36 -> x1, blocking collectives: 358 us -> 82 us  [shards(): table = lax.psum(sketch.reshape(NROW, 128), ('gx', 'gy'))]
    ppermute x36 -> x0, starting transfers between devices: 101 us -> none  [the longest x18 61.4 us: padded_2(): lax.ppermute(tail, axis, [(i, (i + 1) % count) for i in range(ends)])]
    dot_general x190 -> x0, matrix products: 92.9 us -> none  [the longest x32 42.8 us: one_row(): total = jnp.dot(line[None, :], unknowns, precision=exact_mode)[0]]
    another operation x128 -> x0, other arithmetic: 87.4 us -> none
    pallas_call x0 -> x2, Pallas kernels: none -> 56.8 us  [the longest x1 48.8 us: shards(): pl.pallas_call(lambda *refs: basis_kernel(n_gx, n_gy, *refs), out_shape=(...]
    another operation x2 -> x0, loops' own time: 44.2 us -> none  [the longest x1 43.5 us: solve_small(): orthonormal, triangle = lax.fori_loop(0, count, one_column, start)]
    reduce_sum x240 -> x0, other arithmetic: 27 us -> none  [the longest x230 25 us: operate(): jnp.sum(coupling[:, :, None] * shifted[:, :, :, None, :, :], axis=4)]
    another operation x32 -> x1, local copies, waits for them, and re-layouts: 20.9 us -> 0.66 us  [shards(): scales = jnp.broadcast_to(jnp.tile(class_scale, 16)[None, :], (8, 128))]
  transfers between devices with their start and end apart: 36 -> 0, of which waited for: 25 -> 0; matrix products, arithmetic and copies ran while one was open for 1% -> 0% of each run, Pallas kernels for 0% -> 0%
where the time goes in v1:
time: 159 us
  blocking collectives  82 us (52%)
  Pallas kernels  56.8 us (36%)
  local copies, waits for them, and re-layouts  13.2 us (8%)
  other arithmetic  6.24 us (4%)
    psum x1, blocking collectives, shards(): table = lax.psum(sketch.reshape(NROW, 128), ('gx', 'gy'))  82 us
    pallas_call x1, Pallas kernels, shards(): pl.pallas_call(lambda *refs: basis_kernel(n_gx, n_gy, *refs), out_shape=(...  48.8 us
    pallas_call x1, Pallas kernels, shards(): pl.pallas_call(solve_kernel, out_shape=(out, out), in_specs=[vmem] * 3, o...  7.99 us
    unnamed x5, local copies, waits for them, and re-layouts  7.31 us
    select_n x1, other arithmetic, shards(): factor = jnp.where(boundary == 1, jnp.float32(0.0), field)  6.24 us

profile of v1, /device:TPU:1, one launch (start us, length us, event | category | flops | bytes accessed | tf_op | source)
XLA Modules:
  0.0 158.8 jit_solution(2300680471538657769)
XLA Ops:
  0.6 1.6 %fusion = (f32[1]{0:T(128)}, f32[1]{0:T(128)}, f32[1]{0:T(128)}, f32[1]{0:T(128)}, f32[1]{0:T(128)}, /*index=5*/f32[1]{0:T(128)}, f32[1]{0:T(128)}, f32[1]{0:T(128)}) fusion(f32[8]{0:T(128)} %param.11), kind=kLoop, calls=%fused_computation.3 | loop fusion | bytes 64 | tf_op jit(solution)/shard_map/slice | solution.py:348
  2.2 0.7 reshape.20
  2.9 0.1 copy.19
  3.0 0.6 pad.4.refs_7_
  3.7 0.7 tile.2
  4.3 0.1 broadcast_in_dim.45
  4.4 0.6 broadcast_in_dim.46.refs_8_
  5.0 6.2 %select_select_fusion.refs_2_ = f32[2,16,128]{2,1,0:T(8,128)} fusion(s32[2,16,128]{2,1,0:T(8,128)} %param.12, s32[2,16,128]{2,1,0:T(8,128)} %param.13, f32[]{:T(128)} %bitcast.8, f32[]{:T(128)} %bitcast.7, f32[]{:T(128)} %bitcast.6, f32[]{:T(128)} %bitcast.5, f32[]{:T(128)} %bitcast.4, f32[]{:T(128)} %bitcast.3, f32[]{:T(128)} %bitcast.2, f32[]{:T(128)} %bitcast.1), kind=kLoop, calls=%fused_computation.2 | loop fusion | flops 73728 | bytes 49184 | tf_op jit(solution)/shard_map/jit(_where)/select_n | solution.py:349
  11.2 1.4 copy.25
  12.7 0.8 copy.16
  13.5 0.8 reshape.18.refs_0_
  14.2 1.6 %copy.24 = f32[2,16,4,3,128]{4,1,0,3,2:T(8,128)} copy(f32[2,16,4,3,128]{4,2,3,1,0:T(4,128)} %param.9) | data formatting | bytes 393216 | tf_op args[0]
  15.8 48.8 %basis.1 = (f32[9,4,3,2,16,128]{5,4,3,2,1,0:T(8,128)}, f32[9,4,128]{2,1,0:T(4,128)}, f32[8,128]{1,0:T(8,128)}) custom-call(f32[243]{0:T(256)} %reshape.18.refs_0_, f32[4,3,2,16,128]{4,3,2,1,0:T(8,128)} %bitcast.19, f32[2,16,128]{2,1,0:T(8,128)} %select_select_fusion.refs_2_, s32[3,2,16,128]{3,2,1,0:T(8,128)} %bitcast.20, s32[1,128]{1,0:T(1,128)} %bitcast.23, ...), custom_call_target="tpu_custom_call" | custom-call | tf_op jit(solution)/shard_map/basis/pallas_call | solution.py:354
  64.7 0.7 reshape.21
  65.4 82.0 %psum.7.table_ref = f32[36,128]{1,0:T(8,128)} all-reduce(f32[36,128]{1,0:T(8,128)S(1)} %reshape.21), channel_id=1, replica_groups=mesh['gx'=32,'gy'=8] {'gx','gy'}, use_global_device_ids=true, to_apply=%region_0.1 | all-reduce | flops 4608 | bytes 36864 | tf_op jit(solution)/shard_map/psum | solution.py:376
  147.4 8.0 %solve.1 = (f32[4,3,2,16,128]{4,3,2,1,0:T(8,128)}, f32[4,3,2,16,128]{4,3,2,1,0:T(8,128)}) custom-call(f32[36,128]{1,0:T(8,128)} %psum.7.table_ref, f32[8,128]{1,0:T(8,128)} %get-tuple-element.8.shape_ref, f32[9,4,3,2,16,128]{5,4,3,2,1,0:T(8,128)} %get-tuple-element.9.basis_ref), custom_call_target="tpu_custom_call" | custom-call | tf_op jit(solution)/shard_map/solve/pallas_call | solution.py:378
  155.4 1.7 %copy.20 = f32[2,16,4,3,128]{4,2,3,1,0:T(4,128)} copy(f32[2,16,4,3,128]{4,1,0,3,2:T(8,128)} %bitcast.22) | data formatting | bytes 393216
  157.1 1.7 %copy.21 = f32[2,16,4,3,128]{4,2,3,1,0:T(4,128)} copy(f32[2,16,4,3,128]{4,1,0,3,2:T(8,128)} %bitcast.21) | data formatting | bytes 393216

commit v2 on v1

v2 whole, which is shorter than its diff:
```python
import numpy as np
import jax
import jax.numpy as jnp
from jax import lax
from jax.experimental import pallas as pl
from jax.experimental.pallas import tpu as pltpu
from jax.sharding import PartitionSpec as P

STEPS = 8
NCLASS = 8
NV = STEPS + 1
BW = 4
NROW = NV * BW
HIGH = lax.Precision.HIGHEST
MESH = pl.DeviceIdType.MESH

ROW0 = 8


def phase_tables():
    points = [
        (x * np.pi / 3, y * np.pi / 2, z * np.pi / 4)
        for x in range(4)
        for y in range(4)
        for z in range(8)
    ]
    offsets = [(o // 9 - 1, (o // 3) % 3 - 1, o % 3 - 1) for o in range(27)]
    phase = np.zeros((128, 128))
    phase[:27] = np.array(offsets) @ np.array(points).T
    keep = (np.arange(128) < 27)[:, None]
    return (np.cos(phase) * keep).astype(np.float32), (np.sin(phase) * keep).astype(np.float32)


def neighbours(n_gx, n_gy):
    gx, gy = lax.axis_index("gx"), lax.axis_index("gy")
    out = []
    for dx in (-1, 0, 1):
        for dy in (-1, 0, 1):
            if dx == 0 and dy == 0:
                continue
            ok = jnp.bool_(True)
            if dx < 0:
                ok = jnp.logical_and(ok, gx > 0)
            if dx > 0:
                ok = jnp.logical_and(ok, gx < n_gx - 1)
            if dy < 0:
                ok = jnp.logical_and(ok, gy > 0)
            if dy > 0:
                ok = jnp.logical_and(ok, gy < n_gy - 1)
            out.append((dx, dy, ok, {"gx": gx + dx, "gy": gy + dy}))
    return out


def spectrum(cos_ref, sin_ref, coef_ref, scale_ref):
    coef = coef_ref[...]
    re = jnp.dot(coef, cos_ref[...], precision=HIGH, preferred_element_type=jnp.float32)
    im = jnp.dot(coef, sin_ref[...], precision=HIGH, preferred_element_type=jnp.float32)

    def row(t, i, j):
        return t[3 * i + j : 3 * i + j + 1]

    low, high = None, None
    for i in range(3):
        off = jnp.zeros((1, 128), jnp.float32)
        for j in range(3):
            if j != i:
                a = 0.5 * (row(re, i, j) + row(re, j, i))
                b = 0.5 * (row(im, i, j) - row(im, j, i))
                off = off + jnp.sqrt(a * a + b * b)
        lo, hi = row(re, i, i) - off, row(re, i, i) + off
        low = lo if low is None else jnp.minimum(low, lo)
        high = hi if high is None else jnp.maximum(high, hi)
    low = jnp.min(low, axis=1, keepdims=True)
    high = jnp.max(high, axis=1, keepdims=True)
    smin = smax = scale_ref[0]
    for n in range(1, NCLASS):
        smin = jnp.minimum(smin, scale_ref[n])
        smax = jnp.maximum(smax, scale_ref[n])
    low = jnp.minimum(jnp.minimum(low * smin, low * smax), 1.0)
    high = jnp.maximum(high * smax, 1.0)
    span = high - low
    low, high = low + 0.04 * span, high - 0.2 * span
    centre = 0.5 * (low + high)
    half = jnp.maximum(0.5 * (high - low), 1e-3 * high)
    return centre, half


def least_squares(table, ratio, half):
    lane = lax.broadcasted_iota(jnp.int32, (BW, 128), 1)
    row = lax.broadcasted_iota(jnp.int32, (BW, 128), 0)
    none = jnp.float32(0.0)
    rhs = table[0:BW]
    up = jnp.where(lane < BW, none, jnp.where(lane < 2 * BW, jnp.float32(1.0), jnp.float32(0.5)))
    down = jnp.where(lane < NROW, jnp.float32(0.5), none)
    unit = jnp.where(lane == row, jnp.float32(1.0), none)

    def inverse_norm(t):
        return lax.rsqrt(jnp.sum(t * t, axis=1, keepdims=True) + 1e-6)

    scale = inverse_norm(rhs)
    u, p = rhs * scale, unit * scale
    images, coefs = [], []
    for k in range(STEPS):
        d = half * (ratio * p + up * pltpu.roll(p, BW, 1) + down * pltpu.roll(p, 128 - BW, 1))
        image = jnp.dot(d, table, precision=HIGH, preferred_element_type=jnp.float32)
        images.append(image)
        coefs.append(d + pltpu.roll(p, 64, 1))
        if k + 1 < STEPS:
            rest, prest = image, d
            for i in range(BW):
                coupling = jnp.sum(image * u[i : i + 1], axis=1, keepdims=True)
                rest = rest - coupling * u[i : i + 1]
                prest = prest - coupling * p[i : i + 1]
            scale = inverse_norm(rest)
            u, p = rest * scale, prest * scale

    q = jnp.concatenate(images + [rhs], axis=0)
    e = jnp.concatenate(coefs + [unit], axis=0)
    rows = lax.broadcasted_iota(jnp.int32, (NROW, 1), 0)
    lanes = lax.broadcasted_iota(jnp.int32, (1, 128), 1)
    is_rhs = rows >= BW * STEPS
    weight = jnp.zeros((1, 128), jnp.float32)
    square = jnp.zeros((1, 128), jnp.float32)
    along = jnp.zeros((BW, 128), jnp.float32)
    for j in range(BW * STEPS):
        pivot = q[j : j + 1]
        dots = jnp.sum(q * pivot, axis=1, keepdims=True)
        w = 1.0 / (dots[j : j + 1] + 1e-6)
        s = dots[j : j + 1] * w
        here = lanes == j
        weight = weight + jnp.where(here, w, none)
        square = square + jnp.where(here, s, none)
        part = jnp.where(rows > j, dots * w * jnp.where(is_rhs, jnp.float32(1.0), 2.0 - s), none)
        along = along + jnp.where(here, part[BW * STEPS :], none)
        q = q - part * pivot
        e = e - part * e[j : j + 1]
    nq = BW * STEPS
    qs, es, last = q[:nq], e[:nq], e[nq:]
    weight, square, along = weight[:, :nq], square[:, :nq], along[:, :nq]
    first = lane < NROW
    for _ in range(2):
        left = jnp.dot(jnp.where(first, last, none), table, precision=HIGH, preferred_element_type=jnp.float32)
        dots = lax.dot_general(
            left, qs, (((1,), (1,)), ((), ())), precision=HIGH, preferred_element_type=jnp.float32
        )
        change = dots * weight - along * (1.0 - square)
        along = along + change
        last = last - jnp.dot(change, es, precision=HIGH, preferred_element_type=jnp.float32)
    return last


def cycle_kernel(
    n_gx, n_gy, n_y, n_z,
    scale_ref, rhs_ref, stencil_ref, material_ref, boundary_ref, signs_ref, sample_ref, cos_ref, sin_ref,
    solution_ref, residual_ref,
    v, alpha, beta, mask, signed, coef, coef_s, table, rows, weights, part_a, part_b, part_c,
    send_sem, recv_sem, load_sem, sum_send, sum_recv, local_sem,
):
    gx, gy = lax.axis_index("gx"), lax.axis_index("gy")
    around = neighbours(n_gx, n_gy)
    here_y, here_z = gx // n_z, gx % n_z

    groups = (
        (part_a, 0, gy, n_gy, lambda i: {"gx": gx, "gy": i}),
        (part_b, 1, here_y, n_y, lambda i: {"gx": i * n_z + here_z, "gy": gy}),
        (part_c, 2, here_z, n_z, lambda i: {"gx": here_y * n_z + i, "gy": gy}),
    )

    loads = []
    for b in range(BW):
        for c in range(3):
            copy = pltpu.make_async_copy(
                rhs_ref.at[:, :, c, b, :], v.at[0, b, c, pl.ds(1, 2), pl.ds(ROW0, 16), :], load_sem.at[3 * b + c]
            )
            copy.start()
            loads.append(copy)

    barrier = pltpu.get_barrier_semaphore()
    count = jnp.int32(0)
    for dx, dy, ok, device in around:
        count = count + jnp.where(ok, 1, 0)

        @pl.when(ok)
        def _():
            pl.semaphore_signal(barrier, inc=1, device_id=device, device_id_type=MESH)

    for _, _, me, size, device in groups:
        count = count + (size - 1)
        for d in range(1, size):
            pl.semaphore_signal(barrier, inc=1, device_id=device((me + d) % size), device_id_type=MESH)

    def clear(k, carry):
        @pl.when(gx == 0)
        def _():
            v[k, :, :, 0] = jnp.zeros((BW, 3, 32, 128), jnp.float32)

        @pl.when(gx == n_gx - 1)
        def _():
            v[k, :, :, 3] = jnp.zeros((BW, 3, 32, 128), jnp.float32)

        @pl.when(gy == 0)
        def _():
            v[k, :, :, :, ROW0 - 1 : ROW0, :] = jnp.zeros((BW, 3, 4, 1, 128), jnp.float32)

        @pl.when(gy == n_gy - 1)
        def _():
            v[k, :, :, :, ROW0 + 16 : ROW0 + 17, :] = jnp.zeros((BW, 3, 4, 1, 128), jnp.float32)

        return carry

    lax.fori_loop(0, STEPS, clear, 0)
    table[...] = jnp.zeros((128, 128), jnp.float32)
    for copy in loads:
        copy.wait()
    pl.semaphore_wait(barrier, count)

    def halo(k, b, n):
        dx, dy, ok, device = around[n]
        xs = {-1: (1, 1, 3), 0: (1, 2, 1), 1: (2, 1, 0)}[dx]
        ys = {-1: (ROW0, 1, ROW0 + 16), 0: (ROW0, 16, ROW0), 1: (ROW0 + 15, 1, ROW0 - 1)}[dy]
        return pltpu.make_async_remote_copy(
            src_ref=v.at[k, b, :, pl.ds(xs[0], xs[1]), pl.ds(ys[0], ys[1]), :],
            dst_ref=v.at[k, b, :, pl.ds(xs[2], xs[1]), pl.ds(ys[2], ys[1]), :],
            send_sem=send_sem.at[k, b, n],
            recv_sem=recv_sem.at[k, b, n],
            device_id=device,
            device_id_type=MESH,
        )

    def start(k, b):
        for n in range(8):
            @pl.when(around[n][2])
            def _():
                halo(k, b, n).start()

    def arrive(k, b):
        for n in range(8):
            @pl.when(around[n][2])
            def _():
                halo(k, b, 7 - n).wait_recv()

    def sent(k, b):
        for n in range(8):
            @pl.when(around[n][2])
            def _():
                halo(k, b, n).wait_send()

    def piece(group, k, source, d, target):
        buffer, stage, _, _, device = group
        return pltpu.make_async_remote_copy(
            src_ref=buffer.at[k, source],
            dst_ref=buffer.at[k, source],
            send_sem=sum_send.at[stage, k, d],
            recv_sem=sum_recv.at[stage, k, source],
            device_id=device(target),
            device_id_type=MESH,
        )

    def spread(group, k, value):
        buffer, _, me, size, _ = group
        buffer[k, me] = value
        for d in range(1, size):
            piece(group, k, me, d, (me + d) % size).start()

    def gather(group, k):
        buffer, _, me, size, _ = group
        for d in range(1, size):
            source = (me + d) % size
            piece(group, k, source, d, source).wait_recv()
        value = buffer[k, 0]
        for i in range(1, size):
            value = value + buffer[k, i]
        for d in range(1, size):
            piece(group, k, me, d, (me + d) % size).wait_send()
        return value

    def advance(stage, k):
        value = gather(groups[stage], k)
        if stage < 2:
            spread(groups[stage + 1], k, value)
        else:
            table[pl.ds(BW * k, BW), :] = value

    for b in range(BW):
        start(0, b)

    coef[...] = jnp.zeros((16, 128), jnp.float32)
    for i in range(3):
        for j in range(3):
            coef[3 * i + j : 3 * i + j + 1, 0:27] = stencil_ref[i, j : j + 1, :]
    copy = pltpu.make_async_copy(coef, coef_s, local_sem)
    copy.start()
    centre, half = spectrum(cos_ref, sin_ref, coef, scale_ref)
    inverse = 1.0 / half
    inv3 = inverse.reshape(1, 1, 1)
    cen3 = centre.reshape(1, 1, 1)
    material = material_ref[...]
    factor = jnp.zeros((2, 16, 128), jnp.float32)
    for n in range(NCLASS):
        factor = jnp.where(material == n, scale_ref[n], factor)
    fixed = boundary_ref[...] == 1
    alpha[...] = jnp.where(fixed, 0.0, factor * (2.0 * inv3))
    beta[...] = jnp.where(fixed, 2.0 * (1.0 - cen3), -2.0 * cen3) * inv3

    sample = sample_ref[...]
    spot = sample >> 7
    lane = sample & 127
    px = jnp.where(spot >= 48, 1, 0)
    rest = spot - 48 * px
    py = (rest * 171) >> 9
    pc = rest - 3 * py
    mine = pc * 32 + px * 16 + py
    spots = lax.broadcasted_iota(jnp.int32, (96, 128), 0)
    chosen = jnp.where(spots == mine, 1.0, 0.0)
    mask[...] = chosen * np.float32(1.0 / np.sqrt(128.0))
    common = lax.broadcasted_iota(jnp.int32, (128, 128), 0) & lane
    common = common ^ (common >> 4)
    common = common ^ (common >> 2)
    common = common ^ (common >> 1)
    hadamard = (1 - 2 * (common & 1)).astype(jnp.float32)
    signs = jnp.concatenate([signs_ref[x, c] for c in range(3) for x in range(2)], axis=0)
    signs = (2 * signs - 1).astype(jnp.float32)
    picked = lax.dot_general(
        signs, chosen, (((0,), (0,)), ((), ())), precision=HIGH, preferred_element_type=jnp.float32
    )
    signed[...] = hadamard * picked

    def sketch(k):
        out = []
        for b in range(BW):
            block = v[k, b, :, 1:3, ROW0 : ROW0 + 16, :].reshape(96, 128)
            spread_out = jnp.dot(block, signed[...], precision=HIGH, preferred_element_type=jnp.float32)
            out.append(jnp.sum(spread_out * mask[...], axis=0, keepdims=True))
        spread(groups[0], k, jnp.concatenate(out, axis=0))

    sketch(0)
    copy.wait()

    z_lane = lax.broadcasted_iota(jnp.int32, (1, 1, 128), 2)
    not_last = z_lane < 127
    not_first = z_lane > 0

    def step(k, carry):
        first = k == 0
        own = jnp.where(first, jnp.float32(0.5), jnp.float32(1.0))
        old = jnp.where(first, jnp.float32(0.0), jnp.float32(1.0))
        before = jnp.maximum(k - 1, 0)

        def column(b, carry):
            arrive(k, b)
            total = [None, None, None]
            for dz in (-1, 1, 0):
                acc = list(total) if dz == 0 else [None, None, None]
                for dx in (-1, 0, 1):
                    for dy in (-1, 0, 1):
                        offset = 9 * (dx + 1) + 3 * (dy + 1) + (dz + 1)
                        for j in range(3):
                            field = v[k, b, j, pl.ds(1 + dx, 2), pl.ds(ROW0 + dy, 16), :]
                            for i in range(3):
                                term = coef_s[3 * i + j, offset] * field
                                acc[i] = term if acc[i] is None else acc[i] + term
                for i in range(3):
                    if dz == -1:
                        total[i] = jnp.where(not_first, pltpu.roll(acc[i], 1, 2), 0.0)
                    elif dz == 1:
                        total[i] = total[i] + jnp.where(not_last, pltpu.roll(acc[i], 127, 2), 0.0)
                    else:
                        total[i] = acc[i]
            for i in range(3):
                mid = v[k, b, i, 1:3, ROW0 : ROW0 + 16, :]
                last = v[before, b, i, 1:3, ROW0 : ROW0 + 16, :]
                v[k + 1, b, i, 1:3, ROW0 : ROW0 + 16, :] = (
                    own * (alpha[...] * total[i] + beta[...] * mid) - old * last
                )

            @pl.when(k + 1 < STEPS)
            def _():
                start(k + 1, b)

            return carry

        lax.fori_loop(0, BW, column, 0)
        sketch(k + 1)
        advance(0, k)

        @pl.when(k >= 1)
        def _():
            advance(1, k - 1)

        @pl.when(k >= 2)
        def _():
            advance(2, k - 2)

        def drain(b, carry):
            sent(k, b)
            return carry

        lax.fori_loop(0, BW, drain, 0)
        return carry

    lax.fori_loop(0, STEPS, step, 0)
    advance(0, STEPS)
    advance(1, STEPS - 1)
    advance(2, STEPS - 2)
    advance(1, STEPS)
    advance(2, STEPS - 1)
    advance(2, STEPS)

    rows[0:BW] = least_squares(table[...], centre * inverse, half)
    copy = pltpu.make_async_copy(rows, weights, local_sem)
    copy.start()
    copy.wait()

    def combine(b, carry):
        for x in range(2):
            sol = jnp.zeros((3, 16, 128), jnp.float32)
            res = jnp.zeros((3, 16, 128), jnp.float32)
            for k in range(NV):
                for a in range(BW):
                    field = v[k, a, :, 1 + x, ROW0 : ROW0 + 16, :]
                    res = res + weights[b, BW * k + a] * field
                    if k < STEPS:
                        sol = sol - weights[b, 64 + BW * k + a] * field
            solution_ref[b, :, x] = sol
            residual_ref[b, :, x] = res
        return carry

    lax.fori_loop(0, BW, combine, 0)


def solution(mesh):
    n_gx, n_gy = mesh.shape["gx"], mesh.shape["gy"]
    n_z = 8 if n_gx % 8 == 0 else n_gx
    n_y = n_gx // n_z
    cosine, sine = phase_tables()

    def shards(right_side, stencil, class_scale, material, boundary, sign_bits, sample_rows):
        rhs = jnp.transpose(right_side, (0, 1, 3, 2, 4))
        signs = jnp.transpose(sign_bits, (0, 2, 1, 3))
        blocks = jnp.transpose(stencil, (1, 2, 0))
        vmem = pl.BlockSpec(memory_space=pltpu.VMEM)
        smem = pl.BlockSpec(memory_space=pltpu.SMEM)
        hbm = pl.BlockSpec(memory_space=pl.ANY)
        out = jax.ShapeDtypeStruct((BW, 3, 2, 16, 128), jnp.float32)
        most = max(n_gy, n_y, n_z)
        answer, residual = pl.pallas_call(
            lambda *refs: cycle_kernel(n_gx, n_gy, n_y, n_z, *refs),
            out_shape=(out, out),
            in_specs=[smem, hbm] + [vmem] * 7,
            out_specs=(vmem, vmem),
            scratch_shapes=[
                pltpu.VMEM((NV, BW, 3, 4, 32, 128), jnp.float32),
                pltpu.VMEM((2, 16, 128), jnp.float32),
                pltpu.VMEM((2, 16, 128), jnp.float32),
                pltpu.VMEM((96, 128), jnp.float32),
                pltpu.VMEM((128, 128), jnp.float32),
                pltpu.VMEM((16, 128), jnp.float32),
                pltpu.SMEM((16, 128), jnp.float32),
                pltpu.VMEM((128, 128), jnp.float32),
                pltpu.VMEM((8, 128), jnp.float32),
                pltpu.SMEM((8, 128), jnp.float32),
                pltpu.VMEM((NV, n_gy, BW, 128), jnp.float32),
                pltpu.VMEM((NV, n_y, BW, 128), jnp.float32),
                pltpu.VMEM((NV, n_z, BW, 128), jnp.float32),
                pltpu.SemaphoreType.DMA((STEPS, BW, 8)),
                pltpu.SemaphoreType.DMA((STEPS, BW, 8)),
                pltpu.SemaphoreType.DMA((3 * BW,)),
                pltpu.SemaphoreType.DMA((3, NV, most)),
                pltpu.SemaphoreType.DMA((3, NV, most)),
                pltpu.SemaphoreType.DMA,
            ],
            compiler_params=pltpu.CompilerParams(collective_id=0, has_side_effects=True),
            name="cycle",
        )(
            class_scale, rhs, blocks, material, boundary, signs, sample_rows.reshape(1, 128),
            cosine, sine,
        )
        back = lambda t: jnp.transpose(t, (2, 3, 0, 1, 4))
        return back(answer), back(residual)

    return jax.shard_map(
        shards,
        mesh=mesh,
        in_specs=(
            P("gx", "gy", None, None, None),
            P(),
            P(),
            P("gx", "gy", None),
            P("gx", "gy", None),
            P("gx", "gy", None, None),
            P("gx", "gy", None),
        ),
        out_specs=(P("gx", "gy", None, None, None), P("gx", "gy", None, None, None)),
        check_vma=False,
    )
```

time: 159 us -> 80.6 us (0.51)
  blocking collectives: 82 us -> 0 us
  Pallas kernels: 56.8 us -> 77.2 us
  local copies, waits for them, and re-layouts: 13.2 us -> 2.58 us
  other arithmetic: 6.24 us -> 0 us
    psum x1 -> x0, blocking collectives: 82 us -> none  [shards(): table = lax.psum(sketch.reshape(NROW, 128), ('gx', 'gy'))]
    pallas_call x2 -> x1, Pallas kernels: 56.8 us -> 77.2 us  [shards(): pl.pallas_call(lambda *refs: cycle_kernel(n_gx, n_gy, n_y, n_z, *refs), o...]
    select_n x1 -> x0, other arithmetic: 6.24 us -> none  [shards(): factor = jnp.where(boundary == 1, jnp.float32(0.0), field)]
    unnamed x5 -> x4, local copies, waits for them, and re-layouts: 7.31 us -> 2.58 us
    reshape x4 -> x0, local copies, waits for them, and re-layouts: 2.29 us -> none  [the longest x2 0.8 us: shards(): coef = jnp.pad(stencil.reshape(27, 9), ((0, 5), (0, 7)))]
    slice x1 -> x0, local copies, waits for them, and re-layouts: 1.62 us -> none  [shards(): field = jnp.where(material == number, class_scale[number], field)]
where the time goes in v2:
time: 80.6 us; the launch traced here: 80.4 us
  Pallas kernels  77.2 us (96%)
  local copies, waits for them, and re-layouts  2.58 us (3%)
    pallas_call x1, Pallas kernels, shards(): pl.pallas_call(lambda *refs: cycle_kernel(n_gx, n_gy, n_y, n_z, *refs), o...  77.2 us
    unnamed x4, local copies, waits for them, and re-layouts  2.58 us

profile of v2, /device:TPU:1, one launch (start us, length us, event | category | flops | bytes accessed | tf_op | source)
XLA Modules:
  0.0 80.4 jit_solution(4517866549949450979)
XLA Ops:
  0.6 77.2 %cycle.1 = (f32[4,3,2,16,128]{4,3,2,1,0:T(8,128)}, f32[4,3,2,16,128]{4,3,2,1,0:T(8,128)}) custom-call(f32[8]{0:T(128)} %refs_0_.1, f32[2,16,3,4,128]{4,3,2,1,0:T(4,128)} %bitcast.6, f32[3,3,27]{2,1,0:T(4,128)} %bitcast.10, s32[2,16,128]{2,1,0:T(8,128)} %refs_3_.1, s32[2,16,128]{2,1,0:T(8,128)} %refs_4_.1, s32[2,3,16,128]{3,2,1,0:T(8,128)} %bitcast.9, ...), custom_call_target="tpu_custom_call" | custom-call | tf_op jit(solution)/shard_map/cycle/pallas_call | solution.py:446
  77.8 0.0 copy-start
  77.8 1.8 %copy.11 = f32[2,16,4,3,128]{4,2,3,1,0:T(4,128)} copy(f32[2,16,4,3,128]{4,1,0,3,2:T(8,128)} %bitcast.8) | data formatting | bytes 393216
  79.6 0.0 copy-done
  79.6 0.8 %copy.12 = f32[2,16,4,3,128]{4,2,3,1,0:T(4,128)} copy(f32[2,16,4,3,128]{4,1,0,3,2:T(8,128)S(1)} %bitcast.7) | data formatting | bytes 393216
Async XLA Ops:
  77.8 1.8 %copy-start = (f32[4,3,2,16,128]{4,3,2,1,0:T(8,128)S(1)}, f32[4,3,2,16,128]{4,3,2,1,0:T(8,128)}, u32[]{:S(2)}) copy-start(f32[4,3,2,16,128]{4,3,2,1,0:T(8,128)} %get-tuple-element.5) | copy-start | bytes 589828

commit v3 on v2

--- a/solution.py
+++ b/solution.py
@@ -15,6 +15,10 @@
 MESH = pl.DeviceIdType.MESH
 
 ROW0 = 8
+OWN = slice(2, 4)
+PAIRS = STEPS // 2
+GROUPS = PAIRS + 1
+FIXED = -1.0
 
 
 def phase_tables():
@@ -89,10 +93,10 @@
     lane = lax.broadcasted_iota(jnp.int32, (BW, 128), 1)
     row = lax.broadcasted_iota(jnp.int32, (BW, 128), 0)
     none = jnp.float32(0.0)
-    rhs = table[0:BW]
-    up = jnp.where(lane < BW, none, jnp.where(lane < 2 * BW, jnp.float32(1.0), jnp.float32(0.5)))
-    down = jnp.where(lane < NROW, jnp.float32(0.5), none)
-    unit = jnp.where(lane == row, jnp.float32(1.0), none)
+    rhs = table[BW : 2 * BW]
+    up = jnp.where(lane < 2 * BW, none, jnp.where(lane < 3 * BW, jnp.float32(1.0), jnp.float32(0.5)))
+    down = jnp.where(jnp.logical_and(lane >= BW, lane < NROW + BW), jnp.float32(0.5), none)
+    unit = jnp.where(lane == row + BW, jnp.float32(1.0), none)
 
     def inverse_norm(t):
         return lax.rsqrt(jnp.sum(t * t, axis=1, keepdims=True) + 1e-6)
@@ -137,8 +141,8 @@
     nq = BW * STEPS
     qs, es, last = q[:nq], e[:nq], e[nq:]
     weight, square, along = weight[:, :nq], square[:, :nq], along[:, :nq]
-    first = lane < NROW
-    for _ in range(2):
+    first = lane < NROW + BW
+    for _ in range(1):
         left = jnp.dot(jnp.where(first, last, none), table, precision=HIGH, preferred_element_type=jnp.float32)
         dots = lax.dot_general(
             left, qs, (((1,), (1,)), ((), ())), precision=HIGH, preferred_element_type=jnp.float32
@@ -153,8 +157,8 @@
     n_gx, n_gy, n_y, n_z,
     scale_ref, rhs_ref, stencil_ref, material_ref, boundary_ref, signs_ref, sample_ref, cos_ref, sin_ref,
     solution_ref, residual_ref,
-    v, alpha, beta, mask, signed, coef, coef_s, table, rows, weights, part_a, part_b, part_c,
-    send_sem, recv_sem, load_sem, sum_send, sum_recv, local_sem,
+    v, factor, alpha, beta, mask, signed, coef, coef_s, table, rows, weights, part_a, part_b, part_c,
+    send_sem, recv_sem, factor_send, factor_recv, load_sem, sum_send, sum_recv, local_sem,
 ):
     gx, gy = lax.axis_index("gx"), lax.axis_index("gy")
     around = neighbours(n_gx, n_gy)
@@ -170,7 +174,7 @@
     for b in range(BW):
         for c in range(3):
             copy = pltpu.make_async_copy(
-                rhs_ref.at[:, :, c, b, :], v.at[0, b, c, pl.ds(1, 2), pl.ds(ROW0, 16), :], load_sem.at[3 * b + c]
+                rhs_ref.at[:, :, c, b, :], v.at[0, b, c, pl.ds(2, 2), pl.ds(ROW0, 16), :], load_sem.at[3 * b + c]
             )
             copy.start()
             loads.append(copy)
@@ -189,26 +193,50 @@
         for d in range(1, size):
             pl.semaphore_signal(barrier, inc=1, device_id=device((me + d) % size), device_id_type=MESH)
 
-    def clear(k, carry):
+    def clear(t, carry):
+        k = 2 * t
+
         @pl.when(gx == 0)
         def _():
-            v[k, :, :, 0] = jnp.zeros((BW, 3, 32, 128), jnp.float32)
+            v[k, :, :, 0:2] = jnp.zeros((BW, 3, 2, 32, 128), jnp.float32)
 
         @pl.when(gx == n_gx - 1)
         def _():
-            v[k, :, :, 3] = jnp.zeros((BW, 3, 32, 128), jnp.float32)
+            v[k, :, :, 4:6] = jnp.zeros((BW, 3, 2, 32, 128), jnp.float32)
 
         @pl.when(gy == 0)
         def _():
-            v[k, :, :, :, ROW0 - 1 : ROW0, :] = jnp.zeros((BW, 3, 4, 1, 128), jnp.float32)
+            v[k, :, :, :, ROW0 - 2 : ROW0, :] = jnp.zeros((BW, 3, 6, 2, 128), jnp.float32)
 
         @pl.when(gy == n_gy - 1)
         def _():
-            v[k, :, :, :, ROW0 + 16 : ROW0 + 17, :] = jnp.zeros((BW, 3, 4, 1, 128), jnp.float32)
+            v[k, :, :, :, ROW0 + 16 : ROW0 + 18, :] = jnp.zeros((BW, 3, 6, 2, 128), jnp.float32)
 
         return carry
 
-    lax.fori_loop(0, STEPS, clear, 0)
+    lax.fori_loop(0, PAIRS, clear, 0)
+
+    @pl.when(gx == 0)
+    def _():
+        factor[0] = jnp.zeros((32, 128), jnp.float32)
+
+    @pl.when(gx == n_gx - 1)
+    def _():
+        factor[3] = jnp.zeros((32, 128), jnp.float32)
+
+    @pl.when(gy == 0)
+    def _():
+        factor[:, ROW0 - 1 : ROW0, :] = jnp.zeros((4, 1, 128), jnp.float32)
+
+    @pl.when(gy == n_gy - 1)
+    def _():
+        factor[:, ROW0 + 16 : ROW0 + 17, :] = jnp.zeros((4, 1, 128), jnp.float32)
+
+    material = material_ref[...]
+    scales = jnp.zeros((2, 16, 128), jnp.float32)
+    for n in range(NCLASS):
+        scales = jnp.where(material == n, scale_ref[n], scales)
+    factor[1:3, ROW0 : ROW0 + 16, :] = jnp.where(boundary_ref[...] == 1, FIXED, scales)
     table[...] = jnp.zeros((128, 128), jnp.float32)
     for copy in loads:
         copy.wait()
@@ -216,13 +244,26 @@
 
     def halo(k, b, n):
         dx, dy, ok, device = around[n]
+        plane = {-1: 4, 0: 2, 1: 0}[dx]
+        ys = {-1: (ROW0, 2, ROW0 + 16), 0: (ROW0, 16, ROW0), 1: (ROW0 + 14, 2, ROW0 - 2)}[dy]
+        return pltpu.make_async_remote_copy(
+            src_ref=v.at[k, b, :, pl.ds(2, 2), pl.ds(ys[0], ys[1]), :],
+            dst_ref=v.at[k, b, :, pl.ds(plane, 2), pl.ds(ys[2], ys[1]), :],
+            send_sem=send_sem.at[k // 2, b, n],
+            recv_sem=recv_sem.at[k // 2, b, n],
+            device_id=device,
+            device_id_type=MESH,
+        )
+
+    def edge(n):
+        dx, dy, ok, device = around[n]
         xs = {-1: (1, 1, 3), 0: (1, 2, 1), 1: (2, 1, 0)}[dx]
         ys = {-1: (ROW0, 1, ROW0 + 16), 0: (ROW0, 16, ROW0), 1: (ROW0 + 15, 1, ROW0 - 1)}[dy]
         return pltpu.make_async_remote_copy(
-            src_ref=v.at[k, b, :, pl.ds(xs[0], xs[1]), pl.ds(ys[0], ys[1]), :],
-            dst_ref=v.at[k, b, :, pl.ds(xs[2], xs[1]), pl.ds(ys[2], ys[1]), :],
-            send_sem=send_sem.at[k, b, n],
-            recv_sem=recv_sem.at[k, b, n],
+            src_ref=factor.at[pl.ds(xs[0], xs[1]), pl.ds(ys[0], ys[1]), :],
+            dst_ref=factor.at[pl.ds(xs[2], xs[1]), pl.ds(ys[2], ys[1]), :],
+            send_sem=factor_send.at[n],
+            recv_sem=factor_recv.at[n],
             device_id=device,
             device_id_type=MESH,
         )
@@ -279,7 +320,12 @@
         if stage < 2:
             spread(groups[stage + 1], k, value)
         else:
-            table[pl.ds(BW * k, BW), :] = value
+            table[pl.ds(2 * BW * k, 2 * BW), :] = value
+
+    for n in range(8):
+        @pl.when(around[n][2])
+        def _():
+            edge(n).start()
 
     for b in range(BW):
         start(0, b)
@@ -294,14 +340,6 @@
     inverse = 1.0 / half
     inv3 = inverse.reshape(1, 1, 1)
     cen3 = centre.reshape(1, 1, 1)
-    material = material_ref[...]
-    factor = jnp.zeros((2, 16, 128), jnp.float32)
-    for n in range(NCLASS):
-        factor = jnp.where(material == n, scale_ref[n], factor)
-    fixed = boundary_ref[...] == 1
-    alpha[...] = jnp.where(fixed, 0.0, factor * (2.0 * inv3))
-    beta[...] = jnp.where(fixed, 2.0 * (1.0 - cen3), -2.0 * cen3) * inv3
-
     sample = sample_ref[...]
     spot = sample >> 7
     lane = sample & 127
@@ -328,68 +366,93 @@
     def sketch(k):
         out = []
         for b in range(BW):
-            block = v[k, b, :, 1:3, ROW0 : ROW0 + 16, :].reshape(96, 128)
+            block = v[k, b, :, OWN, ROW0 : ROW0 + 16, :].reshape(96, 128)
             spread_out = jnp.dot(block, signed[...], precision=HIGH, preferred_element_type=jnp.float32)
             out.append(jnp.sum(spread_out * mask[...], axis=0, keepdims=True))
-        spread(groups[0], k, jnp.concatenate(out, axis=0))
-
-    sketch(0)
+        return out
+
+    spread(groups[0], 0, jnp.concatenate([jnp.zeros((BW, 128), jnp.float32)] + sketch(0), axis=0))
     copy.wait()
+
+    for n in range(8):
+        @pl.when(around[n][2])
+        def _():
+            edge(7 - n).wait_recv()
+
+    field = factor[...]
+    alpha[...] = jnp.where(field > 0.0, field * (2.0 * inv3), 0.0)
+    beta[...] = jnp.where(
+        field > 0.0, -2.0 * cen3 * inv3, jnp.where(field == FIXED, 2.0 * (1.0 - cen3) * inv3, 0.0)
+    )
 
     z_lane = lax.broadcasted_iota(jnp.int32, (1, 1, 128), 2)
     not_last = z_lane < 127
     not_first = z_lane > 0
 
-    def step(k, carry):
-        first = k == 0
-        own = jnp.where(first, jnp.float32(0.5), jnp.float32(1.0))
-        old = jnp.where(first, jnp.float32(0.0), jnp.float32(1.0))
+    def apply(k, before, b, own, old, plane, row, height):
+        total = [None, None, None]
+        for dz in (-1, 1, 0):
+            acc = list(total) if dz == 0 else [None, None, None]
+            for dx in (-1, 0, 1):
+                for dy in (-1, 0, 1):
+                    offset = 9 * (dx + 1) + 3 * (dy + 1) + (dz + 1)
+                    for j in range(3):
+                        field = v[k, b, j, pl.ds(plane + dx, 2), pl.ds(row + dy, height), :]
+                        for i in range(3):
+                            term = coef_s[3 * i + j, offset] * field
+                            acc[i] = term if acc[i] is None else acc[i] + term
+            for i in range(3):
+                if dz == -1:
+                    total[i] = jnp.where(not_first, pltpu.roll(acc[i], 1, 2), 0.0)
+                elif dz == 1:
+                    total[i] = total[i] + jnp.where(not_last, pltpu.roll(acc[i], 127, 2), 0.0)
+                else:
+                    total[i] = acc[i]
+        a = alpha[pl.ds(plane - 1, 2), row : row + height, :]
+        d = beta[pl.ds(plane - 1, 2), row : row + height, :]
+        for i in range(3):
+            mid = v[k, b, i, pl.ds(plane, 2), row : row + height, :]
+            value = a * total[i] + d * mid
+            if own is not None:
+                last = v[before, b, i, pl.ds(plane, 2), row : row + height, :]
+                value = jnp.where(old, own * value, own * value - last)
+            else:
+                value = value - v[before, b, i, pl.ds(plane, 2), row : row + height, :]
+            v[k + 1, b, i, pl.ds(plane, 2), row : row + height, :] = value
+
+    def pair(t, carry):
+        k = 2 * t
+        start_of = k == 0
+        own = jnp.where(start_of, jnp.float32(0.5), jnp.float32(1.0))
         before = jnp.maximum(k - 1, 0)
 
         def column(b, carry):
             arrive(k, b)
-            total = [None, None, None]
-            for dz in (-1, 1, 0):
-                acc = list(total) if dz == 0 else [None, None, None]
-                for dx in (-1, 0, 1):
-                    for dy in (-1, 0, 1):
-                        offset = 9 * (dx + 1) + 3 * (dy + 1) + (dz + 1)
-                        for j in range(3):
-                            field = v[k, b, j, pl.ds(1 + dx, 2), pl.ds(ROW0 + dy, 16), :]
-                            for i in range(3):
-                                term = coef_s[3 * i + j, offset] * field
-                                acc[i] = term if acc[i] is None else acc[i] + term
-                for i in range(3):
-                    if dz == -1:
-                        total[i] = jnp.where(not_first, pltpu.roll(acc[i], 1, 2), 0.0)
-                    elif dz == 1:
-                        total[i] = total[i] + jnp.where(not_last, pltpu.roll(acc[i], 127, 2), 0.0)
-                    else:
-                        total[i] = acc[i]
-            for i in range(3):
-                mid = v[k, b, i, 1:3, ROW0 : ROW0 + 16, :]
-                last = v[before, b, i, 1:3, ROW0 : ROW0 + 16, :]
-                v[k + 1, b, i, 1:3, ROW0 : ROW0 + 16, :] = (
-                    own * (alpha[...] * total[i] + beta[...] * mid) - old * last
-                )
-
-            @pl.when(k + 1 < STEPS)
+
+            def wide(side, carry):
+                apply(k, before, b, own, start_of, 1 + 2 * side, ROW0 - 1, 24)
+                return carry
+
+            lax.fori_loop(0, 2, wide, 0)
+            apply(k + 1, k, b, None, None, 2, ROW0, 16)
+
+            @pl.when(t + 1 < PAIRS)
             def _():
-                start(k + 1, b)
+                start(k + 2, b)
+
+            @pl.when(b == 1)
+            def _():
+                advance(0, t)
 
             return carry
 
         lax.fori_loop(0, BW, column, 0)
-        sketch(k + 1)
-        advance(0, k)
-
-        @pl.when(k >= 1)
-        def _():
-            advance(1, k - 1)
-
-        @pl.when(k >= 2)
-        def _():
-            advance(2, k - 2)
+        spread(groups[0], t + 1, jnp.concatenate(sketch(k + 1) + sketch(k + 2), axis=0))
+        advance(1, t)
+
+        @pl.when(t >= 1)
+        def _():
+            advance(2, t - 1)
 
         def drain(b, carry):
             sent(k, b)
@@ -398,13 +461,16 @@
         lax.fori_loop(0, BW, drain, 0)
         return carry
 
-    lax.fori_loop(0, STEPS, step, 0)
-    advance(0, STEPS)
-    advance(1, STEPS - 1)
-    advance(2, STEPS - 2)
-    advance(1, STEPS)
-    advance(2, STEPS - 1)
-    advance(2, STEPS)
+    lax.fori_loop(0, PAIRS, pair, 0)
+    for n in range(8):
+        @pl.when(around[n][2])
+        def _():
+            edge(n).wait_send()
+
+    advance(0, PAIRS)
+    advance(2, PAIRS - 1)
+    advance(1, PAIRS)
+    advance(2, PAIRS)
 
     rows[0:BW] = least_squares(table[...], centre * inverse, half)
     copy = pltpu.make_async_copy(rows, weights, local_sem)
@@ -417,10 +483,10 @@
             res = jnp.zeros((3, 16, 128), jnp.float32)
             for k in range(NV):
                 for a in range(BW):
-                    field = v[k, a, :, 1 + x, ROW0 : ROW0 + 16, :]
-                    res = res + weights[b, BW * k + a] * field
+                    field = v[k, a, :, 2 + x, ROW0 : ROW0 + 16, :]
+                    res = res + weights[b, BW * (k + 1) + a] * field
                     if k < STEPS:
-                        sol = sol - weights[b, 64 + BW * k + a] * field
+                        sol = sol - weights[b, 64 + BW * (k + 1) + a] * field
             solution_ref[b, :, x] = sol
             residual_ref[b, :, x] = res
         return carry
@@ -449,9 +515,10 @@
             in_specs=[smem, hbm] + [vmem] * 7,
             out_specs=(vmem, vmem),
             scratch_shapes=[
-                pltpu.VMEM((NV, BW, 3, 4, 32, 128), jnp.float32),
-                pltpu.VMEM((2, 16, 128), jnp.float32),
-                pltpu.VMEM((2, 16, 128), jnp.float32),
+                pltpu.VMEM((NV, BW, 3, 6, 32, 128), jnp.float32),
+                pltpu.VMEM((4, 32, 128), jnp.float32),
+                pltpu.VMEM((4, 32, 128), jnp.float32),
+                pltpu.VMEM((4, 32, 128), jnp.float32),
                 pltpu.VMEM((96, 128), jnp.float32),
                 pltpu.VMEM((128, 128), jnp.float32),
                 pltpu.VMEM((16, 128), jnp.float32),
@@ -459,14 +526,16 @@
                 pltpu.VMEM((128, 128), jnp.float32),
                 pltpu.VMEM((8, 128), jnp.float32),
                 pltpu.SMEM((8, 128), jnp.float32),
-                pltpu.VMEM((NV, n_gy, BW, 128), jnp.float32),
-                pltpu.VMEM((NV, n_y, BW, 128), jnp.float32),
-                pltpu.VMEM((NV, n_z, BW, 128), jnp.float32),
-                pltpu.SemaphoreType.DMA((STEPS, BW, 8)),
-                pltpu.SemaphoreType.DMA((STEPS, BW, 8)),
+                pltpu.VMEM((GROUPS, n_gy, 2 * BW, 128), jnp.float32),
+                pltpu.VMEM((GROUPS, n_y, 2 * BW, 128), jnp.float32),
+                pltpu.VMEM((GROUPS, n_z, 2 * BW, 128), jnp.float32),
+                pltpu.SemaphoreType.DMA((PAIRS, BW, 8)),
+                pltpu.SemaphoreType.DMA((PAIRS, BW, 8)),
+                pltpu.SemaphoreType.DMA((8,)),
+                pltpu.SemaphoreType.DMA((8,)),
                 pltpu.SemaphoreType.DMA((3 * BW,)),
-                pltpu.SemaphoreType.DMA((3, NV, most)),
-                pltpu.SemaphoreType.DMA((3, NV, most)),
+                pltpu.SemaphoreType.DMA((3, GROUPS, most)),
+                pltpu.SemaphoreType.DMA((3, GROUPS, most)),
                 pltpu.SemaphoreType.DMA,
             ],
             compiler_params=pltpu.CompilerParams(collective_id=0, has_side_effects=True),

time: 80.6 us -> 71.1 us (0.88)
  Pallas kernels: 77.2 us -> 67.6 us
    pallas_call x1, Pallas kernels: 77.2 us -> 67.6 us  [shards(): pl.pallas_call(lambda *refs: cycle_kernel(n_gx, n_gy, n_y, n_z, *refs), o...]
where the time goes in v3:
time: 71.1 us; the launch traced here: 70.9 us
  Pallas kernels  67.6 us (95%)
  local copies, waits for them, and re-layouts  2.58 us (4%)
    pallas_call x1, Pallas kernels, shards(): pl.pallas_call(lambda *refs: cycle_kernel(n_gx, n_gy, n_y, n_z, *refs), o...  67.6 us
    unnamed x4, local copies, waits for them, and re-layouts  2.58 us

profile of v3, /device:TPU:1, one launch (start us, length us, event | category | flops | bytes accessed | tf_op | source)
XLA Modules:
  0.0 70.9 jit_solution(7241791962257014936)
XLA Ops:
  0.6 67.6 %cycle.1 = (f32[4,3,2,16,128]{4,3,2,1,0:T(8,128)}, f32[4,3,2,16,128]{4,3,2,1,0:T(8,128)}) custom-call(f32[8]{0:T(128)} %refs_0_.1, f32[2,16,3,4,128]{4,3,2,1,0:T(4,128)} %bitcast.6, f32[3,3,27]{2,1,0:T(4,128)} %bitcast.10, s32[2,16,128]{2,1,0:T(8,128)} %refs_3_.1, s32[2,16,128]{2,1,0:T(8,128)} %refs_4_.1, s32[2,3,16,128]{3,2,1,0:T(8,128)} %bitcast.9, ...), custom_call_target="tpu_custom_call" | custom-call | tf_op jit(solution)/shard_map/cycle/pallas_call | solution.py:512
  68.3 0.0 copy-start
  68.3 1.8 %copy.11 = f32[2,16,4,3,128]{4,2,3,1,0:T(4,128)} copy(f32[2,16,4,3,128]{4,1,0,3,2:T(8,128)} %bitcast.8) | data formatting | bytes 393216
  70.0 0.0 copy-done
  70.1 0.8 %copy.12 = f32[2,16,4,3,128]{4,2,3,1,0:T(4,128)} copy(f32[2,16,4,3,128]{4,1,0,3,2:T(8,128)S(1)} %bitcast.7) | data formatting | bytes 393216
Async XLA Ops:
  68.3 1.8 %copy-start = (f32[4,3,2,16,128]{4,3,2,1,0:T(8,128)S(1)}, f32[4,3,2,16,128]{4,3,2,1,0:T(8,128)}, u32[]{:S(2)}) copy-start(f32[4,3,2,16,128]{4,3,2,1,0:T(8,128)} %get-tuple-element.5) | copy-start | bytes 589828

commit v4 on v3

--- a/solution.py
+++ b/solution.py
@@ -89,75 +89,96 @@
     return centre, half
 
 
-def least_squares(table, ratio, half):
-    lane = lax.broadcasted_iota(jnp.int32, (BW, 128), 1)
-    row = lax.broadcasted_iota(jnp.int32, (BW, 128), 0)
-    none = jnp.float32(0.0)
-    rhs = table[BW : 2 * BW]
-    up = jnp.where(lane < 2 * BW, none, jnp.where(lane < 3 * BW, jnp.float32(1.0), jnp.float32(0.5)))
-    down = jnp.where(jnp.logical_and(lane >= BW, lane < NROW + BW), jnp.float32(0.5), none)
-    unit = jnp.where(lane == row + BW, jnp.float32(1.0), none)
-
-    def inverse_norm(t):
+class LeastSquares:
+    def __init__(self, table, ratio, half):
+        self.ratio, self.half = ratio, half
+        self.lane = lax.broadcasted_iota(jnp.int32, (BW, 128), 1)
+        row = lax.broadcasted_iota(jnp.int32, (BW, 128), 0)
+        none, one, mid = jnp.float32(0.0), jnp.float32(1.0), jnp.float32(0.5)
+        self.rhs = table[BW : 2 * BW]
+        self.up = jnp.where(self.lane < 2 * BW, none, jnp.where(self.lane < 3 * BW, one, mid))
+        self.down = jnp.where(jnp.logical_and(self.lane >= BW, self.lane < NROW + BW), mid, none)
+        self.last = jnp.where(self.lane == row + BW, one, none)
+        scale = self.inverse_norm(self.rhs)
+        self.u, self.p = self.rhs * scale, self.last * scale
+        self.weight = jnp.zeros((1, 128), jnp.float32)
+        self.square = jnp.zeros((1, 128), jnp.float32)
+        self.along = jnp.zeros((BW, 128), jnp.float32)
+        self.q, self.e, self.count = None, None, 0
+
+    def inverse_norm(self, t):
         return lax.rsqrt(jnp.sum(t * t, axis=1, keepdims=True) + 1e-6)
 
-    scale = inverse_norm(rhs)
-    u, p = rhs * scale, unit * scale
-    images, coefs = [], []
-    for k in range(STEPS):
-        d = half * (ratio * p + up * pltpu.roll(p, BW, 1) + down * pltpu.roll(p, 128 - BW, 1))
-        image = jnp.dot(d, table, precision=HIGH, preferred_element_type=jnp.float32)
-        images.append(image)
-        coefs.append(d + pltpu.roll(p, 64, 1))
-        if k + 1 < STEPS:
-            rest, prest = image, d
-            for i in range(BW):
-                coupling = jnp.sum(image * u[i : i + 1], axis=1, keepdims=True)
-                rest = rest - coupling * u[i : i + 1]
-                prest = prest - coupling * p[i : i + 1]
-            scale = inverse_norm(rest)
-            u, p = rest * scale, prest * scale
-
-    q = jnp.concatenate(images + [rhs], axis=0)
-    e = jnp.concatenate(coefs + [unit], axis=0)
-    rows = lax.broadcasted_iota(jnp.int32, (NROW, 1), 0)
-    lanes = lax.broadcasted_iota(jnp.int32, (1, 128), 1)
-    is_rhs = rows >= BW * STEPS
-    weight = jnp.zeros((1, 128), jnp.float32)
-    square = jnp.zeros((1, 128), jnp.float32)
-    along = jnp.zeros((BW, 128), jnp.float32)
-    for j in range(BW * STEPS):
-        pivot = q[j : j + 1]
-        dots = jnp.sum(q * pivot, axis=1, keepdims=True)
-        w = 1.0 / (dots[j : j + 1] + 1e-6)
-        s = dots[j : j + 1] * w
-        here = lanes == j
-        weight = weight + jnp.where(here, w, none)
-        square = square + jnp.where(here, s, none)
-        part = jnp.where(rows > j, dots * w * jnp.where(is_rhs, jnp.float32(1.0), 2.0 - s), none)
-        along = along + jnp.where(here, part[BW * STEPS :], none)
-        q = q - part * pivot
-        e = e - part * e[j : j + 1]
-    nq = BW * STEPS
-    qs, es, last = q[:nq], e[:nq], e[nq:]
-    weight, square, along = weight[:, :nq], square[:, :nq], along[:, :nq]
-    first = lane < NROW + BW
-    for _ in range(1):
-        left = jnp.dot(jnp.where(first, last, none), table, precision=HIGH, preferred_element_type=jnp.float32)
+    def images(self, table, blocks):
+        images, coefs = [], []
+        for k in blocks:
+            p, u = self.p, self.u
+            d = self.half * (self.ratio * p + self.up * pltpu.roll(p, BW, 1) + self.down * pltpu.roll(p, 128 - BW, 1))
+            image = jnp.dot(d, table, precision=HIGH, preferred_element_type=jnp.float32)
+            images.append(image)
+            coefs.append(d + pltpu.roll(p, 64, 1))
+            if k + 1 < STEPS:
+                rest, prest = image, d
+                for i in range(BW):
+                    coupling = jnp.sum(image * u[i : i + 1], axis=1, keepdims=True)
+                    rest = rest - coupling * u[i : i + 1]
+                    prest = prest - coupling * p[i : i + 1]
+                scale = self.inverse_norm(rest)
+                self.u, self.p = rest * scale, prest * scale
+        return images, coefs
+
+    def orthogonalise(self, images, coefs):
+        size = BW * len(images)
+        new, enew = jnp.concatenate(images, axis=0), jnp.concatenate(coefs, axis=0)
+        n = self.count
+        if n:
+            dots = lax.dot_general(
+                new, self.q, (((1,), (1,)), ((), ())), precision=HIGH, preferred_element_type=jnp.float32
+            )
+            dots = dots * (self.weight * (2.0 - self.square))[:, :n]
+            new = new - jnp.dot(dots, self.q, precision=HIGH, preferred_element_type=jnp.float32)
+            enew = enew - jnp.dot(dots, self.e, precision=HIGH, preferred_element_type=jnp.float32)
+        q = jnp.concatenate([new, self.rhs], axis=0)
+        e = jnp.concatenate([enew, self.last], axis=0)
+        rows = lax.broadcasted_iota(jnp.int32, (size + BW, 1), 0)
+        lanes = lax.broadcasted_iota(jnp.int32, (1, 128), 1)
+        is_rhs = rows >= size
+        for j in range(size):
+            pivot = q[j : j + 1]
+            dots = jnp.sum(q * pivot, axis=1, keepdims=True)
+            w = 1.0 / (dots[j : j + 1] + 1e-6)
+            s = dots[j : j + 1] * w
+            here = lanes == n + j
+            self.weight = self.weight + jnp.where(here, w, 0.0)
+            self.square = self.square + jnp.where(here, s, 0.0)
+            part = jnp.where(rows > j, dots * w * jnp.where(is_rhs, jnp.float32(1.0), 2.0 - s), 0.0)
+            self.along = self.along + jnp.where(here, part[size:], 0.0)
+            q = q - part * pivot
+            e = e - part * e[j : j + 1]
+        self.rhs, self.last = q[size:], e[size:]
+        if n:
+            self.q = jnp.concatenate([self.q, q[:size]], axis=0)
+            self.e = jnp.concatenate([self.e, e[:size]], axis=0)
+        else:
+            self.q, self.e = q[:size], e[:size]
+        self.count = n + size
+
+    def refined(self, table):
+        n = self.count
+        here = jnp.where(self.lane < NROW + BW, self.last, 0.0)
+        left = jnp.dot(here, table, precision=HIGH, preferred_element_type=jnp.float32)
         dots = lax.dot_general(
-            left, qs, (((1,), (1,)), ((), ())), precision=HIGH, preferred_element_type=jnp.float32
+            left, self.q, (((1,), (1,)), ((), ())), precision=HIGH, preferred_element_type=jnp.float32
         )
-        change = dots * weight - along * (1.0 - square)
-        along = along + change
-        last = last - jnp.dot(change, es, precision=HIGH, preferred_element_type=jnp.float32)
-    return last
+        change = dots * self.weight[:, :n] - self.along[:, :n] * (1.0 - self.square[:, :n])
+        return self.last - jnp.dot(change, self.e, precision=HIGH, preferred_element_type=jnp.float32)
 
 
 def cycle_kernel(
     n_gx, n_gy, n_y, n_z,
     scale_ref, rhs_ref, stencil_ref, material_ref, boundary_ref, signs_ref, sample_ref, cos_ref, sin_ref,
     solution_ref, residual_ref,
-    v, factor, alpha, beta, mask, signed, coef, coef_s, table, rows, weights, part_a, part_b, part_c,
+    v, factor, alpha, beta, mask, signed, coef, coef_s, table, part_a, part_b, part_c,
     send_sem, recv_sem, factor_send, factor_recv, load_sem, sum_send, sum_recv, local_sem,
 ):
     gx, gy = lax.axis_index("gx"), lax.axis_index("gy")
@@ -467,31 +488,35 @@
         def _():
             edge(n).wait_send()
 
+    least = LeastSquares(table[...], centre * inverse, half)
+    found = least.images(table[...], (0, 1, 2, 3))
     advance(0, PAIRS)
+    least.orthogonalise(*found)
     advance(2, PAIRS - 1)
     advance(1, PAIRS)
+    least.orthogonalise(*least.images(table[...], (4, 5)))
     advance(2, PAIRS)
-
-    rows[0:BW] = least_squares(table[...], centre * inverse, half)
-    copy = pltpu.make_async_copy(rows, weights, local_sem)
-    copy.start()
-    copy.wait()
-
-    def combine(b, carry):
+    least.orthogonalise(*least.images(table[...], (6, 7)))
+    last = least.refined(table[...])
+
+    for b in range(BW):
+
+        def weight(lane):
+            return jnp.broadcast_to(last[b : b + 1, lane : lane + 1], (16, 128))[None]
+
+        sol = [jnp.zeros((3, 16, 128), jnp.float32)] * 2
+        res = [jnp.zeros((3, 16, 128), jnp.float32)] * 2
+        for k in range(NV):
+            for a in range(BW):
+                spot = BW * (k + 1) + a
+                for x in range(2):
+                    field = v[k, a, :, 2 + x, ROW0 : ROW0 + 16, :]
+                    res[x] = res[x] + weight(spot) * field
+                    if k < STEPS:
+                        sol[x] = sol[x] - weight(64 + spot) * field
         for x in range(2):
-            sol = jnp.zeros((3, 16, 128), jnp.float32)
-            res = jnp.zeros((3, 16, 128), jnp.float32)
-            for k in range(NV):
-                for a in range(BW):
-                    field = v[k, a, :, 2 + x, ROW0 : ROW0 + 16, :]
-                    res = res + weights[b, BW * (k + 1) + a] * field
-                    if k < STEPS:
-                        sol = sol - weights[b, 64 + BW * (k + 1) + a] * field
-            solution_ref[b, :, x] = sol
-            residual_ref[b, :, x] = res
-        return carry
-
-    lax.fori_loop(0, BW, combine, 0)
+            solution_ref[b, :, x] = sol[x]
+            residual_ref[b, :, x] = res[x]
 
 
 def solution(mesh):
@@ -507,7 +532,7 @@
         vmem = pl.BlockSpec(memory_space=pltpu.VMEM)
         smem = pl.BlockSpec(memory_space=pltpu.SMEM)
         hbm = pl.BlockSpec(memory_space=pl.ANY)
-        out = jax.ShapeDtypeStruct((BW, 3, 2, 16, 128), jnp.float32)
+        out = pltpu.VMEM((BW, 3, 2, 16, 128), jnp.float32)
         most = max(n_gy, n_y, n_z)
         answer, residual = pl.pallas_call(
             lambda *refs: cycle_kernel(n_gx, n_gy, n_y, n_z, *refs),
@@ -524,8 +549,6 @@
                 pltpu.VMEM((16, 128), jnp.float32),
                 pltpu.SMEM((16, 128), jnp.float32),
                 pltpu.VMEM((128, 128), jnp.float32),
-                pltpu.VMEM((8, 128), jnp.float32),
-                pltpu.SMEM((8, 128), jnp.float32),
                 pltpu.VMEM((GROUPS, n_gy, 2 * BW, 128), jnp.float32),
                 pltpu.VMEM((GROUPS, n_y, 2 * BW, 128), jnp.float32),
                 pltpu.VMEM((GROUPS, n_z, 2 * BW, 128), jnp.float32),

time: 71.1 us -> 65 us (0.914)
  Pallas kernels: 67.6 us -> 62.6 us
  local copies, waits for them, and re-layouts: 2.58 us -> 1.61 us
    pallas_call x1, Pallas kernels: 67.6 us -> 62.6 us  [shards(): pl.pallas_call(lambda *refs: cycle_kernel(n_gx, n_gy, n_y, n_z, *refs), o...]
    unnamed x4 -> x2, local copies, waits for them, and re-layouts: 2.58 us -> 1.61 us
where the time goes in v4:
time: 65 us; the launch traced here: 64.8 us
  Pallas kernels  62.6 us (96%)
  local copies, waits for them, and re-layouts  1.61 us (2%)
    pallas_call x1, Pallas kernels, shards(): pl.pallas_call(lambda *refs: cycle_kernel(n_gx, n_gy, n_y, n_z, *refs), o...  62.6 us
    unnamed x2, local copies, waits for them, and re-layouts  1.61 us

profile of v4, /device:TPU:1, one launch (start us, length us, event | category | flops | bytes accessed | tf_op | source)
XLA Modules:
  0.0 64.8 jit_solution(6747498458243683801)
XLA Ops:
  0.6 62.6 %cycle.1 = (f32[4,3,2,16,128]{4,3,2,1,0:T(8,128)S(1)}, f32[4,3,2,16,128]{4,3,2,1,0:T(8,128)S(1)}) custom-call(f32[8]{0:T(128)} %refs_0_.1, f32[2,16,3,4,128]{4,3,2,1,0:T(4,128)} %bitcast.8, f32[3,3,27]{2,1,0:T(4,128)} %bitcast.10, s32[2,16,128]{2,1,0:T(8,128)} %refs_3_.1, s32[2,16,128]{2,1,0:T(8,128)} %refs_4_.1, s32[2,3,16,128]{3,2,1,0:T(8,128)} %bitcast.9, ...), custom_call_target="tpu_custom_call" | custom-call | tf_op jit(solution)/shard_map/cycle/pallas_call | solution.py:537
  63.2 0.8 %copy.11 = f32[2,16,4,3,128]{4,2,3,1,0:T(4,128)} copy(f32[2,16,4,3,128]{4,1,0,3,2:T(8,128)S(1)} %bitcast.7) | data formatting | bytes 393216
  64.0 0.8 %copy.12 = f32[2,16,4,3,128]{4,2,3,1,0:T(4,128)} copy(f32[2,16,4,3,128]{4,1,0,3,2:T(8,128)S(1)} %bitcast.6) | data formatting | bytes 393216

commit v5 on v4

--- a/solution.py
+++ b/solution.py
@@ -202,17 +202,17 @@
 
     barrier = pltpu.get_barrier_semaphore()
     count = jnp.int32(0)
-    for dx, dy, ok, device in around:
-        count = count + jnp.where(ok, 1, 0)
-
-        @pl.when(ok)
-        def _():
-            pl.semaphore_signal(barrier, inc=1, device_id=device, device_id_type=MESH)
-
-    for _, _, me, size, device in groups:
+    for _, _, me, size, device in reversed(groups):
         count = count + (size - 1)
         for d in range(1, size):
             pl.semaphore_signal(barrier, inc=1, device_id=device((me + d) % size), device_id_type=MESH)
+
+    for dx, dy, ok, device in around:
+        count = count + jnp.where(ok, 1, 0)
+
+        @pl.when(ok)
+        def _():
+            pl.semaphore_signal(barrier, inc=1, device_id=device, device_id_type=MESH)
 
     def clear(t, carry):
         k = 2 * t
@@ -382,15 +382,21 @@
     picked = lax.dot_general(
         signs, chosen, (((0,), (0,)), ((), ())), precision=HIGH, preferred_element_type=jnp.float32
     )
-    signed[...] = hadamard * picked
+    signed[...] = (hadamard * picked).astype(jnp.bfloat16)
 
     def sketch(k):
-        out = []
-        for b in range(BW):
-            block = v[k, b, :, OWN, ROW0 : ROW0 + 16, :].reshape(96, 128)
-            spread_out = jnp.dot(block, signed[...], precision=HIGH, preferred_element_type=jnp.float32)
-            out.append(jnp.sum(spread_out * mask[...], axis=0, keepdims=True))
-        return out
+        block = v[k, :, :, OWN, ROW0 : ROW0 + 16, :].reshape(96 * BW, 128)
+        parts = []
+        for _ in range(3):
+            part = block.astype(jnp.bfloat16)
+            parts.append(part)
+            block = block - part.astype(jnp.float32)
+        found = [jnp.dot(part, signed[...], preferred_element_type=jnp.float32) for part in reversed(parts)]
+        found = (found[0] + found[1]) + found[2]
+        picked = mask[...]
+        return [
+            jnp.sum(found[96 * b : 96 * (b + 1)] * picked, axis=0, keepdims=True) for b in range(BW)
+        ]
 
     spread(groups[0], 0, jnp.concatenate([jnp.zeros((BW, 128), jnp.float32)] + sketch(0), axis=0))
     copy.wait()
@@ -461,7 +467,11 @@
             def _():
                 start(k + 2, b)
 
-            @pl.when(b == 1)
+            @pl.when(jnp.logical_and(b == 1, t >= 1))
+            def _():
+                advance(1, t - 1)
+
+            @pl.when(b == 3)
             def _():
                 advance(0, t)
 
@@ -469,11 +479,10 @@
 
         lax.fori_loop(0, BW, column, 0)
         spread(groups[0], t + 1, jnp.concatenate(sketch(k + 1) + sketch(k + 2), axis=0))
-        advance(1, t)
-
-        @pl.when(t >= 1)
-        def _():
-            advance(2, t - 1)
+
+        @pl.when(t >= 2)
+        def _():
+            advance(2, t - 2)
 
         def drain(b, carry):
             sent(k, b)
@@ -488,12 +497,14 @@
         def _():
             edge(n).wait_send()
 
+    advance(2, PAIRS - 2)
     least = LeastSquares(table[...], centre * inverse, half)
     found = least.images(table[...], (0, 1, 2, 3))
     advance(0, PAIRS)
+    advance(1, PAIRS - 1)
     least.orthogonalise(*found)
+    advance(1, PAIRS)
     advance(2, PAIRS - 1)
-    advance(1, PAIRS)
     least.orthogonalise(*least.images(table[...], (4, 5)))
     advance(2, PAIRS)
     least.orthogonalise(*least.images(table[...], (6, 7)))
@@ -545,7 +556,7 @@
                 pltpu.VMEM((4, 32, 128), jnp.float32),
                 pltpu.VMEM((4, 32, 128), jnp.float32),
                 pltpu.VMEM((96, 128), jnp.float32),
-                pltpu.VMEM((128, 128), jnp.float32),
+                pltpu.VMEM((128, 128), jnp.bfloat16),
                 pltpu.VMEM((16, 128), jnp.float32),
                 pltpu.SMEM((16, 128), jnp.float32),
                 pltpu.VMEM((128, 128), jnp.float32),

time: 65 us -> 64.5 us (level); the launches traced: 64.8 us -> 63.7 us
  Pallas kernels: 62.6 us -> 61.4 us
    pallas_call x1, Pallas kernels: 62.6 us -> 61.4 us  [shards(): pl.pallas_call(lambda *refs: cycle_kernel(n_gx, n_gy, n_y, n_z, *refs), o...]
where the time goes in v5:
time: 64.5 us; the launch traced here: 63.7 us
  Pallas kernels  61.4 us (95%)
  local copies, waits for them, and re-layouts  1.61 us (2%)
    pallas_call x1, Pallas kernels, shards(): pl.pallas_call(lambda *refs: cycle_kernel(n_gx, n_gy, n_y, n_z, *refs), o...  61.4 us
    unnamed x2, local copies, waits for them, and re-layouts  1.61 us

profile of v5, /device:TPU:1, one launch (start us, length us, event | category | flops | bytes accessed | tf_op | source)
XLA Modules:
  0.0 63.7 jit_solution(13075716176768474990)
XLA Ops:
  0.6 61.4 %cycle.1 = (f32[4,3,2,16,128]{4,3,2,1,0:T(8,128)S(1)}, f32[4,3,2,16,128]{4,3,2,1,0:T(8,128)S(1)}) custom-call(f32[8]{0:T(128)} %refs_0_.1, f32[2,16,3,4,128]{4,3,2,1,0:T(4,128)} %bitcast.8, f32[3,3,27]{2,1,0:T(4,128)} %bitcast.10, s32[2,16,128]{2,1,0:T(8,128)} %refs_3_.1, s32[2,16,128]{2,1,0:T(8,128)} %refs_4_.1, s32[2,3,16,128]{3,2,1,0:T(8,128)} %bitcast.9, ...), custom_call_target="tpu_custom_call" | custom-call | tf_op jit(solution)/shard_map/cycle/pallas_call | solution.py:548
  62.0 0.8 %copy.11 = f32[2,16,4,3,128]{4,2,3,1,0:T(4,128)} copy(f32[2,16,4,3,128]{4,1,0,3,2:T(8,128)S(1)} %bitcast.7) | data formatting | bytes 393216
  62.9 0.8 %copy.12 = f32[2,16,4,3,128]{4,2,3,1,0:T(4,128)} copy(f32[2,16,4,3,128]{4,1,0,3,2:T(8,128)S(1)} %bitcast.6) | data formatting | bytes 393216
